TPU v7x, 32 devices: a whole 2x2x4 slice. The times are simulated.
32 devices in a mesh: gx: 8 (over z, core), gy: 4 (over y, x).
Axes of the slice: x: 2, y: 2, z: 4, core: 2. Of those that a mesh axis runs over, the one named last changes fastest.
Arguments:
- green: bfloat16 [8, 4, 1024, 1024], P('gx', 'gy'), may hold values from -0.1875 to 0.1875
- sources: bfloat16 [6, 8, 4, 768, 128], P(None, 'gx', 'gy'), may hold values from -3 to 3
- entering: float32 [8, 4, 1024, 128], P('gx', 'gy'), may hold values from -6 to 6
- start_front: int32 [6], replicated, may hold values from -5 to 5, as said below
Outputs:
- last_traces: float32 [8, 4, 1024, 128], P('gx', 'gy')
Inputs may be any that keep to these rules, and one draw needn't show every extreme that they name: `start_front`: the 6 values are distinct.
All inputs are finite; a program needn't handle non-finite values.
Results may differ from a plain program's by a relative error of at most 0.0055.
Values may be sent and summed in bfloat16 or wider, within the bound.
No kernel may reach another device: no remote copies, remote signals or barrier semaphores. Data moves between devices by JAX's collectives and lax.ppermute only.
A program may use at most 64 MiB of HBM per device.

v0:
```python
import jax
import jax.numpy as jnp
from jax import lax
from jax.sharding import PartitionSpec as P


def passed_along(shard, axis, by):
    size = lax.axis_size(axis)
    pairs = [(i, i + by) for i in range(size) if 0 <= i + by < size]
    return lax.ppermute(shard, axis, pairs)


def local(green, sources, entering, start_front):
    operator = green[0, 0]
    tick_total = sources.shape[0]
    edge_rows = sources.shape[3]
    trace_rows = edge_rows // 2
    corner_rows = operator.shape[0] - edge_rows
    width = entering.shape[3]
    front_index = lax.axis_index("gx") + lax.axis_index("gy")
    rounded = entering[0, 0].astype(jnp.bfloat16)
    corner_zeros = jnp.zeros((corner_rows, width), jnp.float32)
    traces = entering[0, 0]
    for step_index in range(tick_total):
        if step_index > 0:
            outgoing = traces.astype(jnp.bfloat16)
            east_part = outgoing[:trace_rows]
            north_part = outgoing[trace_rows:edge_rows]
            corner_part = outgoing[edge_rows:]
            west_in = passed_along(east_part, "gx", 1)
            south_in = passed_along(north_part, "gy", 1)
            across = passed_along(corner_part, "gx", 1)
            diagonal = passed_along(across, "gy", 1)
            rounded = jnp.concatenate([west_in, south_in, diagonal], axis=0)
        product = jnp.dot(operator, rounded, preferred_element_type=jnp.float32)
        source_term = jnp.concatenate(
            [sources[step_index, 0, 0].astype(jnp.float32), corner_zeros], axis=0
        )
        is_live = jnp.any(start_front == front_index - step_index)
        traces = jnp.where(is_live, product + source_term, jnp.zeros_like(product))
    return traces[None, None]


def solution(mesh):
    in_specs = (
        P("gx", "gy", None, None),
        P(None, "gx", "gy", None, None),
        P("gx", "gy", None, None),
        P(),
    )
    out_specs = P("gx", "gy", None, None)
    return jax.shard_map(local, mesh=mesh, in_specs=in_specs, out_specs=out_specs, check_vma=False)
```

profile of v0, /device:TPU:0, one launch (start us, length us, event | category | flops | bytes accessed | tf_op | source)
XLA Modules:
  0.0 83.3 jit_solution(238099912757264828)
XLA Ops:
  0.0 0.0 copy-start
  0.0 0.0 copy-start.2
  0.0 0.0 copy-start.1
  0.0 1.6 %slice_bitcast_fusion = (bf16[768,128]{1,0:T(8,128)(2,1)S(1)}, bf16[768,128]{1,0:T(8,128)(2,1)S(1)}, bf16[768,128]{1,0:T(8,128)(2,1)S(1)}, bf16[768,128]{1,0:T(8...) fusion(bf16[6,1,1,768,128]{4,3,2,1,0:T(8,128)(2,1)} %param.5), kind=kLoop, calls=%fused_computation.62 | loop fusion | bytes 2359296 | tf_op jit(solution)/shard_map/convert_element_type | solution.py:37
  1.6 0.0 copy-done.2
  1.6 0.8 compare_reduce_fusion.5
  2.4 0.0 copy-done
  2.4 0.0 copy-done.1
  2.4 1.3 %fusion.66 = bf16[1024,128]{1,0:T(8,128)(2,1)S(1)} fusion(bf16[1,1,1024,1024]{3,2,1,0:T(8,128)(2,1)S(1)} %copy-done, bf16[768,128]{1,0:T(8,128)(2,1)S(1)} %get-tuple-element.15, f32[1,1,1024,128]{3,2,1,0:T(8,128)S(1)} %copy-done.1, pred[]{:T(512)} %get-tuple-element.9), kind=kOutput, calls=%fused_computation.30 | convolution fusion | flops 269090816 | bytes 3080193 | tf_op jit(solution)/shard_map/dot_general | solution.py:35
  3.7 2.4 %collective-permute-start.2 = (bf16[256,128]{1,0:T(8,128)(2,1)S(1)}, bf16[256,128]{1,0:T(8,128)(2,1)S(1)}, u32[]{:S(2)}, u32[]{:S(2)}) collective-permute-start(bf16[256,128]{1,0:T(8,128)(2,1)S(1)} %slice.86), channel_id=1, source_target_pairs={{0,4},{4,8},{8,12},{12,16},{16,20},{20,24},{24,28},{1,5},{5,9},{9,... | collective-permute-start | bytes 196616 | tf_op jit(solution)/shard_map/ppermute | solution.py:10
  6.1 4.6 %collective-permute-start = (bf16[384,128]{1,0:T(8,128)(2,1)S(1)}, bf16[384,128]{1,0:T(8,128)(2,1)S(1)}, u32[]{:S(2)}, u32[]{:S(2)}) collective-permute-start(bf16[384,128]{1,0:T(8,128)(2,1)S(1)} %get-tuple-element.25), channel_id=1, source_target_pairs={{0,4},{4,8},{8,12},{12,16},{16,20},{20,24},{24,28},{1,5},{5,9},{9,... | collective-permute-start | bytes 294920 | tf_op jit(solution)/shard_map/ppermute | solution.py:10
  10.7 3.4 %collective-permute-start.1 = (bf16[384,128]{1,0:T(8,128)(2,1)S(1)}, bf16[384,128]{1,0:T(8,128)(2,1)S(1)}, u32[]{:S(2)}, u32[]{:S(2)}) collective-permute-start(bf16[384,128]{1,0:T(8,128)(2,1)S(1)} %get-tuple-element.26), channel_id=1, source_target_pairs={{0,1},{1,2},{2,3},{4,5},{5,6},{6,7},{8,9},{9,10},{10,11},{12,13},{... | collective-permute-start | bytes 294920 | tf_op jit(solution)/shard_map/ppermute | solution.py:10
  14.1 0.0 collective-permute-done.2
  14.2 3.4 %collective-permute-start.3 = (bf16[256,128]{1,0:T(8,128)(2,1)S(1)}, bf16[256,128]{1,0:T(8,128)(2,1)S(1)}, u32[]{:S(2)}, u32[]{:S(2)}) collective-permute-start(bf16[256,128]{1,0:T(8,128)(2,1)S(1)} %collective-permute-done.2), channel_id=1, source_target_pairs={{0,1},{1,2},{2,3},{4,5},{5,6},{6,7},{8,9},{9,10},{10,11},{12,13},{... | collective-permute-start | bytes 196616 | tf_op jit(solution)/shard_map/ppermute | solution.py:10
  17.6 0.0 collective-permute-done
  17.6 0.0 collective-permute-done.1
  17.6 1.9 %collective-permute-done.3 = bf16[256,128]{1,0:T(8,128)(2,1)S(1)} collective-permute-done((bf16[256,128]{1,0:T(8,128)(2,1)S(1)}, bf16[256,128]{1,0:T(8,128)(2,1)S(1)}, u32[]{:S(2)}, u32[]{:S(2)}) %collective-permute-start.3) | collective-permute-done | bytes 65568 | tf_op jit(solution)/shard_map/ppermute | solution.py:10
  19.5 1.3 %fusion.78 = bf16[1024,128]{1,0:T(8,128)(2,1)S(1)} fusion(bf16[1,1,1024,1024]{3,2,1,0:T(8,128)(2,1)S(1)} %copy-done, bf16[256,128]{1,0:T(8,128)(2,1)S(1)} %collective-permute-done.3, bf16[384,128]{1,0:T(8,128)(2,1)S(1)} %collective-permute-done.1, bf16[384,128]{1,0:T(8,128)(2,1)S(1)} %collective-permute-done, bf16[768,128]{1,0:T(8,128)(2,1)S(1)} %get-tuple-element.14, ...), kind=kOutput, calls=%fused_computation.34 | convolution fusion | flops 269746176 | bytes 2818049 | tf_op jit(solution)/shard_map/dot_general | solution.py:35
  20.8 1.3 %collective-permute-start.6 = (bf16[256,128]{1,0:T(8,128)(2,1)S(1)}, bf16[256,128]{1,0:T(8,128)(2,1)S(1)}, u32[]{:S(2)}, u32[]{:S(2)}) collective-permute-start(bf16[256,128]{1,0:T(8,128)(2,1)S(1)} %slice.89), channel_id=1, source_target_pairs={{0,4},{4,8},{8,12},{12,16},{16,20},{20,24},{24,28},{1,5},{5,9},{9,... | collective-permute-start | bytes 196616 | tf_op jit(solution)/shard_map/ppermute | solution.py:10
  22.1 4.2 %collective-permute-start.4 = (bf16[384,128]{1,0:T(8,128)(2,1)S(1)}, bf16[384,128]{1,0:T(8,128)(2,1)S(1)}, u32[]{:S(2)}, u32[]{:S(2)}) collective-permute-start(bf16[384,128]{1,0:T(8,128)(2,1)S(1)} %get-tuple-element.23), channel_id=1, source_target_pairs={{0,4},{4,8},{8,12},{12,16},{16,20},{20,24},{24,28},{1,5},{5,9},{9,... | collective-permute-start | bytes 294920 | tf_op jit(solution)/shard_map/ppermute | solution.py:10
  26.4 4.3 %collective-permute-start.5 = (bf16[384,128]{1,0:T(8,128)(2,1)S(1)}, bf16[384,128]{1,0:T(8,128)(2,1)S(1)}, u32[]{:S(2)}, u32[]{:S(2)}) collective-permute-start(bf16[384,128]{1,0:T(8,128)(2,1)S(1)} %get-tuple-element.24), channel_id=1, source_target_pairs={{0,1},{1,2},{2,3},{4,5},{5,6},{6,7},{8,9},{9,10},{10,11},{12,13},{... | collective-permute-start | bytes 294920 | tf_op jit(solution)/shard_map/ppermute | solution.py:10
  30.6 0.0 collective-permute-done.6
  30.6 4.3 %collective-permute-start.7 = (bf16[256,128]{1,0:T(8,128)(2,1)S(1)}, bf16[256,128]{1,0:T(8,128)(2,1)S(1)}, u32[]{:S(2)}, u32[]{:S(2)}) collective-permute-start(bf16[256,128]{1,0:T(8,128)(2,1)S(1)} %collective-permute-done.6), channel_id=1, source_target_pairs={{0,1},{1,2},{2,3},{4,5},{5,6},{6,7},{8,9},{9,10},{10,11},{12,13},{... | collective-permute-start | bytes 196616 | tf_op jit(solution)/shard_map/ppermute | solution.py:10
  35.0 0.0 collective-permute-done.4
  35.0 0.0 collective-permute-done.5
  35.0 1.9 %collective-permute-done.7 = bf16[256,128]{1,0:T(8,128)(2,1)S(1)} collective-permute-done((bf16[256,128]{1,0:T(8,128)(2,1)S(1)}, bf16[256,128]{1,0:T(8,128)(2,1)S(1)}, u32[]{:S(2)}, u32[]{:S(2)}) %collective-permute-start.7) | collective-permute-done | bytes 65568 | tf_op jit(solution)/shard_map/ppermute | solution.py:10
  36.8 1.4 %fusion.75 = bf16[1024,128]{1,0:T(8,128)(2,1)S(1)} fusion(bf16[1,1,1024,1024]{3,2,1,0:T(8,128)(2,1)S(1)} %copy-done, bf16[256,128]{1,0:T(8,128)(2,1)S(1)} %collective-permute-done.7, bf16[384,128]{1,0:T(8,128)(2,1)S(1)} %collective-permute-done.5, bf16[384,128]{1,0:T(8,128)(2,1)S(1)} %collective-permute-done.4, bf16[768,128]{1,0:T(8,128)(2,1)S(1)} %get-tuple-element.13, ...), kind=kOutput, calls=%fused_computation.33 | convolution fusion | flops 269746176 | bytes 2818049 | tf_op jit(solution)/shard_map/dot_general | solution.py:35
  38.2 1.3 %collective-permute-start.10 = (bf16[256,128]{1,0:T(8,128)(2,1)S(1)}, bf16[256,128]{1,0:T(8,128)(2,1)S(1)}, u32[]{:S(2)}, u32[]{:S(2)}) collective-permute-start(bf16[256,128]{1,0:T(8,128)(2,1)S(1)} %slice.92), channel_id=1, source_target_pairs={{0,4},{4,8},{8,12},{12,16},{16,20},{20,24},{24,28},{1,5},{5,9},{9,... | collective-permute-start | bytes 196616 | tf_op jit(solution)/shard_map/ppermute | solution.py:10
  39.5 4.2 %collective-permute-start.8 = (bf16[384,128]{1,0:T(8,128)(2,1)S(1)}, bf16[384,128]{1,0:T(8,128)(2,1)S(1)}, u32[]{:S(2)}, u32[]{:S(2)}) collective-permute-start(bf16[384,128]{1,0:T(8,128)(2,1)S(1)} %get-tuple-element.21), channel_id=1, source_target_pairs={{0,4},{4,8},{8,12},{12,16},{16,20},{20,24},{24,28},{1,5},{5,9},{9,... | collective-permute-start | bytes 294920 | tf_op jit(solution)/shard_map/ppermute | solution.py:10
  43.8 4.3 %collective-permute-start.9 = (bf16[384,128]{1,0:T(8,128)(2,1)S(1)}, bf16[384,128]{1,0:T(8,128)(2,1)S(1)}, u32[]{:S(2)}, u32[]{:S(2)}) collective-permute-start(bf16[384,128]{1,0:T(8,128)(2,1)S(1)} %get-tuple-element.22), channel_id=1, source_target_pairs={{0,1},{1,2},{2,3},{4,5},{5,6},{6,7},{8,9},{9,10},{10,11},{12,13},{... | collective-permute-start | bytes 294920 | tf_op jit(solution)/shard_map/ppermute | solution.py:10
  48.0 0.0 collective-permute-done.10
  48.0 2.8 %collective-permute-start.11 = (bf16[256,128]{1,0:T(8,128)(2,1)S(1)}, bf16[256,128]{1,0:T(8,128)(2,1)S(1)}, u32[]{:S(2)}, u32[]{:S(2)}) collective-permute-start(bf16[256,128]{1,0:T(8,128)(2,1)S(1)} %collective-permute-done.10), channel_id=1, source_target_pairs={{0,1},{1,2},{2,3},{4,5},{5,6},{6,7},{8,9},{9,10},{10,11},{12,13},{... | collective-permute-start | bytes 196616 | tf_op jit(solution)/shard_map/ppermute | solution.py:10
  50.9 0.0 collective-permute-done.8
  50.9 0.0 collective-permute-done.9
  50.9 1.9 %collective-permute-done.11 = bf16[256,128]{1,0:T(8,128)(2,1)S(1)} collective-permute-done((bf16[256,128]{1,0:T(8,128)(2,1)S(1)}, bf16[256,128]{1,0:T(8,128)(2,1)S(1)}, u32[]{:S(2)}, u32[]{:S(2)}) %collective-permute-start.11) | collective-permute-done | bytes 65568 | tf_op jit(solution)/shard_map/ppermute | solution.py:10
  52.8 1.3 %fusion.72 = bf16[1024,128]{1,0:T(8,128)(2,1)S(1)} fusion(bf16[1,1,1024,1024]{3,2,1,0:T(8,128)(2,1)S(1)} %copy-done, bf16[256,128]{1,0:T(8,128)(2,1)S(1)} %collective-permute-done.11, bf16[384,128]{1,0:T(8,128)(2,1)S(1)} %collective-permute-done.9, bf16[384,128]{1,0:T(8,128)(2,1)S(1)} %collective-permute-done.8, ...), kind=kOutput, calls=%fused_computation.32 | convolution fusion | flops 269746176 | bytes 2818049 | tf_op jit(solution)/shard_map/dot_general | solution.py:35
  54.1 1.3 %collective-permute-start.14 = (bf16[256,128]{1,0:T(8,128)(2,1)S(1)}, bf16[256,128]{1,0:T(8,128)(2,1)S(1)}, u32[]{:S(2)}, u32[]{:S(2)}) collective-permute-start(bf16[256,128]{1,0:T(8,128)(2,1)S(1)} %slice.95), channel_id=1, source_target_pairs={{0,4},{4,8},{8,12},{12,16},{16,20},{20,24},{24,28},{1,5},{5,9},{9,... | collective-permute-start | bytes 196616 | tf_op jit(solution)/shard_map/ppermute | solution.py:10
  55.4 2.5 %collective-permute-start.12 = (bf16[384,128]{1,0:T(8,128)(2,1)S(1)}, bf16[384,128]{1,0:T(8,128)(2,1)S(1)}, u32[]{:S(2)}, u32[]{:S(2)}) collective-permute-start(bf16[384,128]{1,0:T(8,128)(2,1)S(1)} %get-tuple-element.19), channel_id=1, source_target_pairs={{0,4},{4,8},{8,12},{12,16},{16,20},{20,24},{24,28},{1,5},{5,9},{9,... | collective-permute-start | bytes 294920 | tf_op jit(solution)/shard_map/ppermute | solution.py:10
  57.9 4.3 %collective-permute-start.13 = (bf16[384,128]{1,0:T(8,128)(2,1)S(1)}, bf16[384,128]{1,0:T(8,128)(2,1)S(1)}, u32[]{:S(2)}, u32[]{:S(2)}) collective-permute-start(bf16[384,128]{1,0:T(8,128)(2,1)S(1)} %get-tuple-element.20), channel_id=1, source_target_pairs={{0,1},{1,2},{2,3},{4,5},{5,6},{6,7},{8,9},{9,10},{10,11},{12,13},{... | collective-permute-start | bytes 294920 | tf_op jit(solution)/shard_map/ppermute | solution.py:10
  62.2 0.0 collective-permute-done.14
  62.2 2.8 %collective-permute-start.15 = (bf16[256,128]{1,0:T(8,128)(2,1)S(1)}, bf16[256,128]{1,0:T(8,128)(2,1)S(1)}, u32[]{:S(2)}, u32[]{:S(2)}) collective-permute-start(bf16[256,128]{1,0:T(8,128)(2,1)S(1)} %collective-permute-done.14), channel_id=1, source_target_pairs={{0,1},{1,2},{2,3},{4,5},{5,6},{6,7},{8,9},{9,10},{10,11},{12,13},{... | collective-permute-start | bytes 196616 | tf_op jit(solution)/shard_map/ppermute | solution.py:10
  65.0 0.0 collective-permute-done.12
  65.1 0.0 collective-permute-done.13
  65.1 1.9 %collective-permute-done.15 = bf16[256,128]{1,0:T(8,128)(2,1)S(1)} collective-permute-done((bf16[256,128]{1,0:T(8,128)(2,1)S(1)}, bf16[256,128]{1,0:T(8,128)(2,1)S(1)}, u32[]{:S(2)}, u32[]{:S(2)}) %collective-permute-start.15) | collective-permute-done | bytes 65568 | tf_op jit(solution)/shard_map/ppermute | solution.py:10
  66.9 1.3 %fusion.69 = bf16[1024,128]{1,0:T(8,128)(2,1)S(1)} fusion(bf16[1,1,1024,1024]{3,2,1,0:T(8,128)(2,1)S(1)} %copy-done, bf16[256,128]{1,0:T(8,128)(2,1)S(1)} %collective-permute-done.15, bf16[384,128]{1,0:T(8,128)(2,1)S(1)} %collective-permute-done.13, bf16[384,128]{1,0:T(8,128)(2,1)S(1)} %collective-permute-done.12, ...), kind=kOutput, calls=%fused_computation.31 | convolution fusion | flops 269746176 | bytes 2818049 | tf_op jit(solution)/shard_map/dot_general | solution.py:35
  68.3 1.3 %collective-permute-start.18 = (bf16[256,128]{1,0:T(8,128)(2,1)S(1)}, bf16[256,128]{1,0:T(8,128)(2,1)S(1)}, u32[]{:S(2)}, u32[]{:S(2)}) collective-permute-start(bf16[256,128]{1,0:T(8,128)(2,1)S(1)} %slice.98), channel_id=1, source_target_pairs={{0,4},{4,8},{8,12},{12,16},{16,20},{20,24},{24,28},{1,5},{5,9},{9,... | collective-permute-start | bytes 196616 | tf_op jit(solution)/shard_map/ppermute | solution.py:10
  69.6 2.5 %collective-permute-start.16 = (bf16[384,128]{1,0:T(8,128)(2,1)S(1)}, bf16[384,128]{1,0:T(8,128)(2,1)S(1)}, u32[]{:S(2)}, u32[]{:S(2)}) collective-permute-start(bf16[384,128]{1,0:T(8,128)(2,1)S(1)} %get-tuple-element.17), channel_id=1, source_target_pairs={{0,4},{4,8},{8,12},{12,16},{16,20},{20,24},{24,28},{1,5},{5,9},{9,... | collective-permute-start | bytes 294920 | tf_op jit(solution)/shard_map/ppermute | solution.py:10
  72.2 4.3 %collective-permute-start.17 = (bf16[384,128]{1,0:T(8,128)(2,1)S(1)}, bf16[384,128]{1,0:T(8,128)(2,1)S(1)}, u32[]{:S(2)}, u32[]{:S(2)}) collective-permute-start(bf16[384,128]{1,0:T(8,128)(2,1)S(1)} %get-tuple-element.18), channel_id=1, source_target_pairs={{0,1},{1,2},{2,3},{4,5},{5,6},{6,7},{8,9},{9,10},{10,11},{12,13},{... | collective-permute-start | bytes 294920 | tf_op jit(solution)/shard_map/ppermute | solution.py:10
  76.4 0.0 collective-permute-done.18
  76.5 2.8 %collective-permute-start.19 = (bf16[256,128]{1,0:T(8,128)(2,1)S(1)}, bf16[256,128]{1,0:T(8,128)(2,1)S(1)}, u32[]{:S(2)}, u32[]{:S(2)}) collective-permute-start(bf16[256,128]{1,0:T(8,128)(2,1)S(1)} %collective-permute-done.18), channel_id=1, source_target_pairs={{0,1},{1,2},{2,3},{4,5},{5,6},{6,7},{8,9},{9,10},{10,11},{12,13},{... | collective-permute-start | bytes 196616 | tf_op jit(solution)/shard_map/ppermute | solution.py:10
  79.3 0.0 collective-permute-done.16
  79.3 0.0 collective-permute-done.17
  79.3 1.9 %collective-permute-done.19 = bf16[256,128]{1,0:T(8,128)(2,1)S(1)} collective-permute-done((bf16[256,128]{1,0:T(8,128)(2,1)S(1)}, bf16[256,128]{1,0:T(8,128)(2,1)S(1)}, u32[]{:S(2)}, u32[]{:S(2)}) %collective-permute-start.19) | collective-permute-done | bytes 65568 | tf_op jit(solution)/shard_map/ppermute | solution.py:10
  81.2 2.1 %fusion.57 = f32[1,1,1024,128]{3,2,1,0:T(8,128)} fusion(bf16[1,1,1024,1024]{3,2,1,0:T(8,128)(2,1)S(1)} %copy-done, bf16[256,128]{1,0:T(8,128)(2,1)S(1)} %collective-permute-done.19, bf16[384,128]{1,0:T(8,128)(2,1)S(1)} %collective-permute-done.17, bf16[384,128]{1,0:T(8,128)(2,1)S(1)} %collective-permute-done.16, ...), kind=kOutput, calls=%fused_computation.27 | convolution fusion | flops 269615104 | bytes 3080193 | tf_op jit(solution)/shard_map/dot_general | solution.py:35
  (10 shorter events, 0.1 us)
Async XLA Ops:
  0.0 2.4 %copy-start = (bf16[1,1,1024,1024]{3,2,1,0:T(8,128)(2,1)S(1)}, bf16[1,1,1024,1024]{3,2,1,0:T(8,128)(2,1)}, u32[]{:S(2)}) copy-start(bf16[1,1,1024,1024]{3,2,1,0:T(8,128)(2,1)} %param.4) | copy-start | bytes 6291460
  0.0 1.6 %copy-start.2 = (s32[6]{0:T(128)S(1)}, s32[6]{0:T(128)}, u32[]{:S(2)}) copy-start(s32[6]{0:T(128)} %param.7) | copy-start | bytes 76
  0.0 2.4 %copy-start.1 = (f32[1,1,1024,128]{3,2,1,0:T(8,128)S(1)}, f32[1,1,1024,128]{3,2,1,0:T(8,128)}, u32[]{:S(2)}) copy-start(f32[1,1,1024,128]{3,2,1,0:T(8,128)} %param.6) | copy-start | bytes 1572868
  3.7 10.4 %collective-permute-start.2 = (bf16[256,128]{1,0:T(8,128)(2,1)S(1)}, bf16[256,128]{1,0:T(8,128)(2,1)S(1)}, u32[]{:S(2)}, u32[]{:S(2)}) collective-permute-start(bf16[256,128]{1,0:T(8,128)(2,1)S(1)} %slice.86), channel_id=1, source_target_pairs={{0,4},{4,8},{8,12},{12,16},{16,20},{20,24},{24,28},{1,5},{5,9},{9,... | collective-permute-start | bytes 196616 | tf_op jit(solution)/shard_map/ppermute | solution.py:10
  6.1 11.4 %collective-permute-start = (bf16[384,128]{1,0:T(8,128)(2,1)S(1)}, bf16[384,128]{1,0:T(8,128)(2,1)S(1)}, u32[]{:S(2)}, u32[]{:S(2)}) collective-permute-start(bf16[384,128]{1,0:T(8,128)(2,1)S(1)} %get-tuple-element.25), channel_id=1, source_target_pairs={{0,4},{4,8},{8,12},{12,16},{16,20},{20,24},{24,28},{1,5},{5,9},{9,... | collective-permute-start | bytes 294920 | tf_op jit(solution)/shard_map/ppermute | solution.py:10
  10.7 6.8 %collective-permute-start.1 = (bf16[384,128]{1,0:T(8,128)(2,1)S(1)}, bf16[384,128]{1,0:T(8,128)(2,1)S(1)}, u32[]{:S(2)}, u32[]{:S(2)}) collective-permute-start(bf16[384,128]{1,0:T(8,128)(2,1)S(1)} %get-tuple-element.26), channel_id=1, source_target_pairs={{0,1},{1,2},{2,3},{4,5},{5,6},{6,7},{8,9},{9,10},{10,11},{12,13},{... | collective-permute-start | bytes 294920 | tf_op jit(solution)/shard_map/ppermute | solution.py:10
  14.2 5.3 %collective-permute-start.3 = (bf16[256,128]{1,0:T(8,128)(2,1)S(1)}, bf16[256,128]{1,0:T(8,128)(2,1)S(1)}, u32[]{:S(2)}, u32[]{:S(2)}) collective-permute-start(bf16[256,128]{1,0:T(8,128)(2,1)S(1)} %collective-permute-done.2), channel_id=1, source_target_pairs={{0,1},{1,2},{2,3},{4,5},{5,6},{6,7},{8,9},{9,10},{10,11},{12,13},{... | collective-permute-start | bytes 196616 | tf_op jit(solution)/shard_map/ppermute | solution.py:10
  20.8 9.8 %collective-permute-start.6 = (bf16[256,128]{1,0:T(8,128)(2,1)S(1)}, bf16[256,128]{1,0:T(8,128)(2,1)S(1)}, u32[]{:S(2)}, u32[]{:S(2)}) collective-permute-start(bf16[256,128]{1,0:T(8,128)(2,1)S(1)} %slice.89), channel_id=1, source_target_pairs={{0,4},{4,8},{8,12},{12,16},{16,20},{20,24},{24,28},{1,5},{5,9},{9,... | collective-permute-start | bytes 196616 | tf_op jit(solution)/shard_map/ppermute | solution.py:10
  22.1 12.8 %collective-permute-start.4 = (bf16[384,128]{1,0:T(8,128)(2,1)S(1)}, bf16[384,128]{1,0:T(8,128)(2,1)S(1)}, u32[]{:S(2)}, u32[]{:S(2)}) collective-permute-start(bf16[384,128]{1,0:T(8,128)(2,1)S(1)} %get-tuple-element.23), channel_id=1, source_target_pairs={{0,4},{4,8},{8,12},{12,16},{16,20},{20,24},{24,28},{1,5},{5,9},{9,... | collective-permute-start | bytes 294920 | tf_op jit(solution)/shard_map/ppermute | solution.py:10
  26.4 8.6 %collective-permute-start.5 = (bf16[384,128]{1,0:T(8,128)(2,1)S(1)}, bf16[384,128]{1,0:T(8,128)(2,1)S(1)}, u32[]{:S(2)}, u32[]{:S(2)}) collective-permute-start(bf16[384,128]{1,0:T(8,128)(2,1)S(1)} %get-tuple-element.24), channel_id=1, source_target_pairs={{0,1},{1,2},{2,3},{4,5},{5,6},{6,7},{8,9},{9,10},{10,11},{12,13},{... | collective-permute-start | bytes 294920 | tf_op jit(solution)/shard_map/ppermute | solution.py:10
  30.6 6.2 %collective-permute-start.7 = (bf16[256,128]{1,0:T(8,128)(2,1)S(1)}, bf16[256,128]{1,0:T(8,128)(2,1)S(1)}, u32[]{:S(2)}, u32[]{:S(2)}) collective-permute-start(bf16[256,128]{1,0:T(8,128)(2,1)S(1)} %collective-permute-done.6), channel_id=1, source_target_pairs={{0,1},{1,2},{2,3},{4,5},{5,6},{6,7},{8,9},{9,10},{10,11},{12,13},{... | collective-permute-start | bytes 196616 | tf_op jit(solution)/shard_map/ppermute | solution.py:10
  38.2 9.8 %collective-permute-start.10 = (bf16[256,128]{1,0:T(8,128)(2,1)S(1)}, bf16[256,128]{1,0:T(8,128)(2,1)S(1)}, u32[]{:S(2)}, u32[]{:S(2)}) collective-permute-start(bf16[256,128]{1,0:T(8,128)(2,1)S(1)} %slice.92), channel_id=1, source_target_pairs={{0,4},{4,8},{8,12},{12,16},{16,20},{20,24},{24,28},{1,5},{5,9},{9,... | collective-permute-start | bytes 196616 | tf_op jit(solution)/shard_map/ppermute | solution.py:10
  39.5 11.3 %collective-permute-start.8 = (bf16[384,128]{1,0:T(8,128)(2,1)S(1)}, bf16[384,128]{1,0:T(8,128)(2,1)S(1)}, u32[]{:S(2)}, u32[]{:S(2)}) collective-permute-start(bf16[384,128]{1,0:T(8,128)(2,1)S(1)} %get-tuple-element.21), channel_id=1, source_target_pairs={{0,4},{4,8},{8,12},{12,16},{16,20},{20,24},{24,28},{1,5},{5,9},{9,... | collective-permute-start | bytes 294920 | tf_op jit(solution)/shard_map/ppermute | solution.py:10
  43.8 7.1 %collective-permute-start.9 = (bf16[384,128]{1,0:T(8,128)(2,1)S(1)}, bf16[384,128]{1,0:T(8,128)(2,1)S(1)}, u32[]{:S(2)}, u32[]{:S(2)}) collective-permute-start(bf16[384,128]{1,0:T(8,128)(2,1)S(1)} %get-tuple-element.22), channel_id=1, source_target_pairs={{0,1},{1,2},{2,3},{4,5},{5,6},{6,7},{8,9},{9,10},{10,11},{12,13},{... | collective-permute-start | bytes 294920 | tf_op jit(solution)/shard_map/ppermute | solution.py:10
  48.0 4.7 %collective-permute-start.11 = (bf16[256,128]{1,0:T(8,128)(2,1)S(1)}, bf16[256,128]{1,0:T(8,128)(2,1)S(1)}, u32[]{:S(2)}, u32[]{:S(2)}) collective-permute-start(bf16[256,128]{1,0:T(8,128)(2,1)S(1)} %collective-permute-done.10), channel_id=1, source_target_pairs={{0,1},{1,2},{2,3},{4,5},{5,6},{6,7},{8,9},{9,10},{10,11},{12,13},{... | collective-permute-start | bytes 196616 | tf_op jit(solution)/shard_map/ppermute | solution.py:10
  54.1 8.2 %collective-permute-start.14 = (bf16[256,128]{1,0:T(8,128)(2,1)S(1)}, bf16[256,128]{1,0:T(8,128)(2,1)S(1)}, u32[]{:S(2)}, u32[]{:S(2)}) collective-permute-start(bf16[256,128]{1,0:T(8,128)(2,1)S(1)} %slice.95), channel_id=1, source_target_pairs={{0,4},{4,8},{8,12},{12,16},{16,20},{20,24},{24,28},{1,5},{5,9},{9,... | collective-permute-start | bytes 196616 | tf_op jit(solution)/shard_map/ppermute | solution.py:10
  55.4 9.7 %collective-permute-start.12 = (bf16[384,128]{1,0:T(8,128)(2,1)S(1)}, bf16[384,128]{1,0:T(8,128)(2,1)S(1)}, u32[]{:S(2)}, u32[]{:S(2)}) collective-permute-start(bf16[384,128]{1,0:T(8,128)(2,1)S(1)} %get-tuple-element.19), channel_id=1, source_target_pairs={{0,4},{4,8},{8,12},{12,16},{16,20},{20,24},{24,28},{1,5},{5,9},{9,... | collective-permute-start | bytes 294920 | tf_op jit(solution)/shard_map/ppermute | solution.py:10
  57.9 7.1 %collective-permute-start.13 = (bf16[384,128]{1,0:T(8,128)(2,1)S(1)}, bf16[384,128]{1,0:T(8,128)(2,1)S(1)}, u32[]{:S(2)}, u32[]{:S(2)}) collective-permute-start(bf16[384,128]{1,0:T(8,128)(2,1)S(1)} %get-tuple-element.20), channel_id=1, source_target_pairs={{0,1},{1,2},{2,3},{4,5},{5,6},{6,7},{8,9},{9,10},{10,11},{12,13},{... | collective-permute-start | bytes 294920 | tf_op jit(solution)/shard_map/ppermute | solution.py:10
  62.2 4.7 %collective-permute-start.15 = (bf16[256,128]{1,0:T(8,128)(2,1)S(1)}, bf16[256,128]{1,0:T(8,128)(2,1)S(1)}, u32[]{:S(2)}, u32[]{:S(2)}) collective-permute-start(bf16[256,128]{1,0:T(8,128)(2,1)S(1)} %collective-permute-done.14), channel_id=1, source_target_pairs={{0,1},{1,2},{2,3},{4,5},{5,6},{6,7},{8,9},{9,10},{10,11},{12,13},{... | collective-permute-start | bytes 196616 | tf_op jit(solution)/shard_map/ppermute | solution.py:10
  68.3 8.2 %collective-permute-start.18 = (bf16[256,128]{1,0:T(8,128)(2,1)S(1)}, bf16[256,128]{1,0:T(8,128)(2,1)S(1)}, u32[]{:S(2)}, u32[]{:S(2)}) collective-permute-start(bf16[256,128]{1,0:T(8,128)(2,1)S(1)} %slice.98), channel_id=1, source_target_pairs={{0,4},{4,8},{8,12},{12,16},{16,20},{20,24},{24,28},{1,5},{5,9},{9,... | collective-permute-start | bytes 196616 | tf_op jit(solution)/shard_map/ppermute | solution.py:10
  69.6 9.7 %collective-permute-start.16 = (bf16[384,128]{1,0:T(8,128)(2,1)S(1)}, bf16[384,128]{1,0:T(8,128)(2,1)S(1)}, u32[]{:S(2)}, u32[]{:S(2)}) collective-permute-start(bf16[384,128]{1,0:T(8,128)(2,1)S(1)} %get-tuple-element.17), channel_id=1, source_target_pairs={{0,4},{4,8},{8,12},{12,16},{16,20},{20,24},{24,28},{1,5},{5,9},{9,... | collective-permute-start | bytes 294920 | tf_op jit(solution)/shard_map/ppermute | solution.py:10
  72.2 7.1 %collective-permute-start.17 = (bf16[384,128]{1,0:T(8,128)(2,1)S(1)}, bf16[384,128]{1,0:T(8,128)(2,1)S(1)}, u32[]{:S(2)}, u32[]{:S(2)}) collective-permute-start(bf16[384,128]{1,0:T(8,128)(2,1)S(1)} %get-tuple-element.18), channel_id=1, source_target_pairs={{0,1},{1,2},{2,3},{4,5},{5,6},{6,7},{8,9},{9,10},{10,11},{12,13},{... | collective-permute-start | bytes 294920 | tf_op jit(solution)/shard_map/ppermute | solution.py:10
  76.5 4.7 %collective-permute-start.19 = (bf16[256,128]{1,0:T(8,128)(2,1)S(1)}, bf16[256,128]{1,0:T(8,128)(2,1)S(1)}, u32[]{:S(2)}, u32[]{:S(2)}) collective-permute-start(bf16[256,128]{1,0:T(8,128)(2,1)S(1)} %collective-permute-done.18), channel_id=1, source_target_pairs={{0,1},{1,2},{2,3},{4,5},{5,6},{6,7},{8,9},{9,10},{10,11},{12,13},{... | collective-permute-start | bytes 196616 | tf_op jit(solution)/shard_map/ppermute | solution.py:10
where the time goes:
time: 84 us; the launch traced here: 83.3 us
  starting transfers between devices  62.3 us (74%)
  waiting for transfers between devices  9.36 us (11%)
  matrix products  8.77 us (10%)
  local copies, waits for them, and re-layouts  1.68 us (2%)
    ppermute x20, starting transfers between devices, passed_along(): return lax.ppermute(shard, axis, pairs)  62.3 us
    ppermute x20, waiting for transfers between devices, passed_along(): return lax.ppermute(shard, axis, pairs)  9.36 us
    dot_general x6, matrix products, local(): product = jnp.dot(operator, rounded, preferred_element_type=jnp.float32)  8.77 us
  transfers between devices with their start and end apart: 20, of which 5 were waited for; matrix products, arithmetic and copies ran while one was open for 0% of the time, Pallas kernels for 0%

commit v1 on v0

v1 whole, which is shorter than its diff:
```python
import jax
import jax.numpy as jnp
from jax import lax
from jax.sharding import PartitionSpec as P

AXES = ("gx", "gy")


def passed_along(shard, dx, dy):
    nx, ny = lax.axis_size("gx"), lax.axis_size("gy")
    pairs = [
        (i * ny + j, (i + dx) % nx * ny + (j + dy) % ny)
        for i in range(nx)
        for j in range(ny)
    ]
    return lax.ppermute(shard, AXES, pairs)


def local(green, sources, entering, start_front):
    operator = green[0, 0]
    tick_total = sources.shape[0]
    edge_rows = sources.shape[3]
    trace_rows = edge_rows // 2
    corner_rows = operator.shape[0] - edge_rows
    width = entering.shape[3]
    column, row = lax.axis_index("gx"), lax.axis_index("gy")
    front_index = column + row
    rounded = entering[0, 0].astype(jnp.bfloat16)
    corner_zeros = jnp.zeros((corner_rows, width), jnp.float32)
    traces = entering[0, 0]

    def kept(arrived, inside):
        return jnp.where(inside, arrived, jnp.zeros_like(arrived))

    for step_index in range(tick_total):
        if step_index > 0:
            outgoing = traces.astype(jnp.bfloat16)
            diagonal = passed_along(outgoing[edge_rows:], 1, 1)
            west_in = passed_along(outgoing[:trace_rows], 1, 0)
            south_in = passed_along(outgoing[trace_rows:edge_rows], 0, 1)
            rounded = jnp.concatenate(
                [
                    kept(west_in, column > 0),
                    kept(south_in, row > 0),
                    kept(diagonal, (column > 0) & (row > 0)),
                ],
                axis=0,
            )
        product = jnp.dot(operator, rounded, preferred_element_type=jnp.float32)
        source_term = jnp.concatenate(
            [sources[step_index, 0, 0].astype(jnp.float32), corner_zeros], axis=0
        )
        is_live = jnp.any(start_front == front_index - step_index)
        traces = jnp.where(is_live, product + source_term, jnp.zeros_like(product))
    return traces[None, None]


def solution(mesh):
    in_specs = (
        P("gx", "gy", None, None),
        P(None, "gx", "gy", None, None),
        P("gx", "gy", None, None),
        P(),
    )
    out_specs = P("gx", "gy", None, None)
    return jax.shard_map(local, mesh=mesh, in_specs=in_specs, out_specs=out_specs, check_vma=False)
```

time: 84 us -> 54.8 us (0.65)
  starting transfers between devices: 62.3 us -> 19 us
  waiting for transfers between devices: 9.36 us -> 22.4 us
  matrix products: 8.77 us -> 9.73 us
    ppermute x20 -> x15, starting transfers between devices: 62.3 us -> 19 us  [passed_along(): return lax.ppermute(shard, AXES, pairs)]
    ppermute x20 -> x15, waiting for transfers between devices: 9.36 us -> 22.4 us  [passed_along(): return lax.ppermute(shard, AXES, pairs)]
    dot_general x6, matrix products: 8.77 us -> 9.73 us  [local(): product = jnp.dot(operator, rounded, preferred_element_type=jnp.float32)]
  transfers between devices with their start and end apart: 20 -> 15, of which waited for: 5 -> 11; matrix products, arithmetic and copies ran while one was open for 0% -> 0% of each run, Pallas kernels for 0% -> 0%
where the time goes in v1:
time: 54.8 us; the launch traced here: 54.6 us
  waiting for transfers between devices  22.4 us (41%)
  starting transfers between devices  19 us (35%)
  matrix products  9.73 us (18%)
  local copies, waits for them, and re-layouts  2.35 us (4%)
  other arithmetic  0.94 us (2%)
    ppermute x15, waiting for transfers between devices, passed_along(): return lax.ppermute(shard, AXES, pairs)  22.4 us
    ppermute x15, starting transfers between devices, passed_along(): return lax.ppermute(shard, AXES, pairs)  19 us
    dot_general x6, matrix products, local(): product = jnp.dot(operator, rounded, preferred_element_type=jnp.float32)  9.73 us
    convert_element_type x1, local copies, waits for them, and re-layouts, local(): sources[step_index, 0, 0].astype(jnp.float32)  2.24 us
  transfers between devices with their start and end apart: 15, of which 11 were waited for; matrix products, arithmetic and copies ran while one was open for 0% of the time, Pallas kernels for 0%

profile of v1, /device:TPU:0, one launch (start us, length us, event | category | flops | bytes accessed | tf_op | source)
XLA Modules:
  0.0 54.6 jit_solution(15368924924496197349)
XLA Ops:
  0.0 0.0 copy-start
  0.0 0.0 copy-start.2
  0.0 0.0 copy-start.1
  0.0 2.2 %slice_bitcast_fusion = (bf16[768,128]{1,0:T(8,128)(2,1)S(1)}, bf16[768,128]{1,0:T(8,128)(2,1)S(1)}, bf16[768,128]{1,0:T(8,128)(2,1)S(1)}, bf16[768,128]{1,0:T(8...) fusion(bf16[6,1,1,768,128]{4,3,2,1,0:T(8,128)(2,1)} %param.5), kind=kLoop, calls=%fused_computation.62 | loop fusion | bytes 2359296 | tf_op jit(solution)/shard_map/convert_element_type | solution.py:51
  2.2 0.0 copy-done.2
  2.2 0.8 %compare_reduce_fusion.5 = (pred[]{:T(512)}, pred[]{:T(512)}, pred[]{:T(512)}, pred[]{:T(512)}, pred[]{:T(512)}, /*index=5*/pred[]{:T(512)}) fusion(s32[6]{0:T(128)S(1)} %copy-done.2, s32[]{:T(128)S(6)} %sub.15, s32[]{:T(128)S(6)} %sub.18, s32[]{:T(128)S(6)} %sub.17, s32[]{:T(128)S(6)} %sub.16, s32[]{:T(128)S(6)} %add.38, s32[]{:T(128)S(6)} %sub.19), kind=kLoop, calls=%fused_computation.88 | loop fusion | flops 66 | bytes 54 | tf_op jit(solution)/shard_map/reduce_or | solution.py:53
  3.0 0.0 copy-done
  3.0 0.0 copy-done.1
  3.0 1.3 %fusion.66 = bf16[1024,128]{1,0:T(8,128)(2,1)S(1)} fusion(bf16[1,1,1024,1024]{3,2,1,0:T(8,128)(2,1)S(1)} %copy-done, bf16[768,128]{1,0:T(8,128)(2,1)S(1)} %get-tuple-element.15, f32[1,1,1024,128]{3,2,1,0:T(8,128)S(1)} %copy-done.1, pred[]{:T(512)} %get-tuple-element.9), kind=kOutput, calls=%fused_computation.30 | convolution fusion | flops 269090816 | bytes 3080193 | tf_op jit(solution)/shard_map/dot_general | solution.py:49
  4.4 2.5 %collective-permute-start.2 = (bf16[256,128]{1,0:T(8,128)(2,1)S(1)}, bf16[256,128]{1,0:T(8,128)(2,1)S(1)}, u32[]{:S(2)}, u32[]{:S(2)}) collective-permute-start(bf16[256,128]{1,0:T(8,128)(2,1)S(1)} %slice.86), channel_id=1, source_target_pairs={{0,5},{1,6},{2,7},{3,4},{4,9},{5,10},{6,11},{7,8},{8,13},{9,14},{1... | collective-permute-start | bytes 196616 | tf_op jit(solution)/shard_map/ppermute | solution.py:16
  6.9 1.7 %collective-permute-start = (bf16[384,128]{1,0:T(8,128)(2,1)S(1)}, bf16[384,128]{1,0:T(8,128)(2,1)S(1)}, u32[]{:S(2)}, u32[]{:S(2)}) collective-permute-start(bf16[384,128]{1,0:T(8,128)(2,1)S(1)} %get-tuple-element.25), channel_id=1, source_target_pairs={{0,4},{1,5},{2,6},{3,7},{4,8},{5,9},{6,10},{7,11},{8,12},{9,13},{1... | collective-permute-start | bytes 294920 | tf_op jit(solution)/shard_map/ppermute | solution.py:16
  8.6 1.5 %collective-permute-start.1 = (bf16[384,128]{1,0:T(8,128)(2,1)S(1)}, bf16[384,128]{1,0:T(8,128)(2,1)S(1)}, u32[]{:S(2)}, u32[]{:S(2)}) collective-permute-start(bf16[384,128]{1,0:T(8,128)(2,1)S(1)} %get-tuple-element.26), channel_id=1, source_target_pairs={{0,1},{1,2},{2,3},{3,0},{4,5},{5,6},{6,7},{7,4},{8,9},{9,10},{10,1... | collective-permute-start | bytes 294920 | tf_op jit(solution)/shard_map/ppermute | solution.py:16
  10.1 2.8 %collective-permute-done.2 = bf16[256,128]{1,0:T(8,128)(2,1)S(1)} collective-permute-done((bf16[256,128]{1,0:T(8,128)(2,1)S(1)}, bf16[256,128]{1,0:T(8,128)(2,1)S(1)}, u32[]{:S(2)}, u32[]{:S(2)}) %collective-permute-start.2) | collective-permute-done | bytes 65568 | tf_op jit(solution)/shard_map/ppermute | solution.py:16
  12.9 0.5 collective-permute-done
  13.4 1.5 %collective-permute-done.1 = bf16[384,128]{1,0:T(8,128)(2,1)S(1)} collective-permute-done((bf16[384,128]{1,0:T(8,128)(2,1)S(1)}, bf16[384,128]{1,0:T(8,128)(2,1)S(1)}, u32[]{:S(2)}, u32[]{:S(2)}) %collective-permute-start.1) | collective-permute-done | bytes 98336 | tf_op jit(solution)/shard_map/ppermute | solution.py:16
  14.9 2.3 %fusion.78 = bf16[1024,128]{1,0:T(8,128)(2,1)S(1)} fusion(bf16[1,1,1024,1024]{3,2,1,0:T(8,128)(2,1)S(1)} %copy-done, bf16[256,128]{1,0:T(8,128)(2,1)S(1)} %broadcast_select_fusion.14, bf16[384,128]{1,0:T(8,128)(2,1)S(1)} %broadcast_select_fusion.4, bf16[384,128]{1,0:T(8,128)(2,1)S(1)} %broadcast_select_fusion.9, bf16[768,128]{1,0:T(8,128)(2,1)} %get-tuple-element.14, ...), kind=kOutput, calls=%fused_computation.34 | convolution fusion | flops 269746176 | bytes 2818049 | tf_op jit(solution)/shard_map/dot_general | solution.py:49
  17.2 0.1 collective-permute-start.5
  17.3 1.1 %collective-permute-start.3 = (bf16[384,128]{1,0:T(8,128)(2,1)S(1)}, bf16[384,128]{1,0:T(8,128)(2,1)S(1)}, u32[]{:S(2)}, u32[]{:S(2)}) collective-permute-start(bf16[384,128]{1,0:T(8,128)(2,1)S(1)} %get-tuple-element.23), channel_id=1, source_target_pairs={{0,4},{1,5},{2,6},{3,7},{4,8},{5,9},{6,10},{7,11},{8,12},{9,13},{1... | collective-permute-start | bytes 294920 | tf_op jit(solution)/shard_map/ppermute | solution.py:16
  18.4 2.4 %collective-permute-start.4 = (bf16[384,128]{1,0:T(8,128)(2,1)S(1)}, bf16[384,128]{1,0:T(8,128)(2,1)S(1)}, u32[]{:S(2)}, u32[]{:S(2)}) collective-permute-start(bf16[384,128]{1,0:T(8,128)(2,1)S(1)} %get-tuple-element.24), channel_id=1, source_target_pairs={{0,1},{1,2},{2,3},{3,0},{4,5},{5,6},{6,7},{7,4},{8,9},{9,10},{10,1... | collective-permute-start | bytes 294920 | tf_op jit(solution)/shard_map/ppermute | solution.py:16
  20.8 3.8 %collective-permute-done.5 = bf16[256,128]{1,0:T(8,128)(2,1)S(1)} collective-permute-done((bf16[256,128]{1,0:T(8,128)(2,1)S(1)}, bf16[256,128]{1,0:T(8,128)(2,1)S(1)}, u32[]{:S(2)}, u32[]{:S(2)}) %collective-permute-start.5) | collective-permute-done | bytes 65568 | tf_op jit(solution)/shard_map/ppermute | solution.py:16
  24.7 0.0 collective-permute-done.3
  24.7 0.1 collective-permute-done.4
  24.8 1.4 %fusion.75 = bf16[1024,128]{1,0:T(8,128)(2,1)S(1)} fusion(bf16[1,1,1024,1024]{3,2,1,0:T(8,128)(2,1)S(1)} %copy-done, bf16[256,128]{1,0:T(8,128)(2,1)S(1)} %broadcast_select_fusion.13, bf16[384,128]{1,0:T(8,128)(2,1)S(1)} %broadcast_select_fusion.3, bf16[384,128]{1,0:T(8,128)(2,1)S(1)} %broadcast_select_fusion.8, ...), kind=kOutput, calls=%fused_computation.33 | convolution fusion | flops 269746176 | bytes 2818049 | tf_op jit(solution)/shard_map/dot_general | solution.py:49
  26.2 1.0 %collective-permute-start.8 = (bf16[256,128]{1,0:T(8,128)(2,1)S(1)}, bf16[256,128]{1,0:T(8,128)(2,1)S(1)}, u32[]{:S(2)}, u32[]{:S(2)}) collective-permute-start(bf16[256,128]{1,0:T(8,128)(2,1)S(1)} %slice.92), channel_id=1, source_target_pairs={{0,5},{1,6},{2,7},{3,4},{4,9},{5,10},{6,11},{7,8},{8,13},{9,14},{1... | collective-permute-start | bytes 196616 | tf_op jit(solution)/shard_map/ppermute | solution.py:16
  27.2 1.0 %collective-permute-start.6 = (bf16[384,128]{1,0:T(8,128)(2,1)S(1)}, bf16[384,128]{1,0:T(8,128)(2,1)S(1)}, u32[]{:S(2)}, u32[]{:S(2)}) collective-permute-start(bf16[384,128]{1,0:T(8,128)(2,1)S(1)} %get-tuple-element.21), channel_id=1, source_target_pairs={{0,4},{1,5},{2,6},{3,7},{4,8},{5,9},{6,10},{7,11},{8,12},{9,13},{1... | collective-permute-start | bytes 294920 | tf_op jit(solution)/shard_map/ppermute | solution.py:16
  28.2 1.6 %collective-permute-start.7 = (bf16[384,128]{1,0:T(8,128)(2,1)S(1)}, bf16[384,128]{1,0:T(8,128)(2,1)S(1)}, u32[]{:S(2)}, u32[]{:S(2)}) collective-permute-start(bf16[384,128]{1,0:T(8,128)(2,1)S(1)} %get-tuple-element.22), channel_id=1, source_target_pairs={{0,1},{1,2},{2,3},{3,0},{4,5},{5,6},{6,7},{7,4},{8,9},{9,10},{10,1... | collective-permute-start | bytes 294920 | tf_op jit(solution)/shard_map/ppermute | solution.py:16
  29.9 3.8 %collective-permute-done.8 = bf16[256,128]{1,0:T(8,128)(2,1)S(1)} collective-permute-done((bf16[256,128]{1,0:T(8,128)(2,1)S(1)}, bf16[256,128]{1,0:T(8,128)(2,1)S(1)}, u32[]{:S(2)}, u32[]{:S(2)}) %collective-permute-start.8) | collective-permute-done | bytes 65568 | tf_op jit(solution)/shard_map/ppermute | solution.py:16
  33.7 0.1 collective-permute-done.6
  33.8 0.8 %collective-permute-done.7 = bf16[384,128]{1,0:T(8,128)(2,1)S(1)} collective-permute-done((bf16[384,128]{1,0:T(8,128)(2,1)S(1)}, bf16[384,128]{1,0:T(8,128)(2,1)S(1)}, u32[]{:S(2)}, u32[]{:S(2)}) %collective-permute-start.7) | collective-permute-done | bytes 98336 | tf_op jit(solution)/shard_map/ppermute | solution.py:16
  34.6 1.3 %fusion.72 = bf16[1024,128]{1,0:T(8,128)(2,1)S(1)} fusion(bf16[1,1,1024,1024]{3,2,1,0:T(8,128)(2,1)S(1)} %copy-done, bf16[256,128]{1,0:T(8,128)(2,1)S(1)} %broadcast_select_fusion.12, bf16[384,128]{1,0:T(8,128)(2,1)S(1)} %broadcast_select_fusion.2, bf16[384,128]{1,0:T(8,128)(2,1)S(1)} %broadcast_select_fusion.7, ...), kind=kOutput, calls=%fused_computation.32 | convolution fusion | flops 269746176 | bytes 2818049 | tf_op jit(solution)/shard_map/dot_general | solution.py:49
  36.0 0.1 collective-permute-start.11
  36.1 0.9 %collective-permute-start.9 = (bf16[384,128]{1,0:T(8,128)(2,1)S(1)}, bf16[384,128]{1,0:T(8,128)(2,1)S(1)}, u32[]{:S(2)}, u32[]{:S(2)}) collective-permute-start(bf16[384,128]{1,0:T(8,128)(2,1)S(1)} %get-tuple-element.19), channel_id=1, source_target_pairs={{0,4},{1,5},{2,6},{3,7},{4,8},{5,9},{6,10},{7,11},{8,12},{9,13},{1... | collective-permute-start | bytes 294920 | tf_op jit(solution)/shard_map/ppermute | solution.py:16
  37.0 1.9 %collective-permute-start.10 = (bf16[384,128]{1,0:T(8,128)(2,1)S(1)}, bf16[384,128]{1,0:T(8,128)(2,1)S(1)}, u32[]{:S(2)}, u32[]{:S(2)}) collective-permute-start(bf16[384,128]{1,0:T(8,128)(2,1)S(1)} %get-tuple-element.20), channel_id=1, source_target_pairs={{0,1},{1,2},{2,3},{3,0},{4,5},{5,6},{6,7},{7,4},{8,9},{9,10},{10,1... | collective-permute-start | bytes 294920 | tf_op jit(solution)/shard_map/ppermute | solution.py:16
  38.9 4.5 %collective-permute-done.11 = bf16[256,128]{1,0:T(8,128)(2,1)S(1)} collective-permute-done((bf16[256,128]{1,0:T(8,128)(2,1)S(1)}, bf16[256,128]{1,0:T(8,128)(2,1)S(1)}, u32[]{:S(2)}, u32[]{:S(2)}) %collective-permute-start.11) | collective-permute-done | bytes 65568 | tf_op jit(solution)/shard_map/ppermute | solution.py:16
  43.4 0.0 collective-permute-done.9
  43.4 0.0 collective-permute-done.10
  43.4 1.3 %fusion.69 = bf16[1024,128]{1,0:T(8,128)(2,1)S(1)} fusion(bf16[1,1,1024,1024]{3,2,1,0:T(8,128)(2,1)S(1)} %copy-done, bf16[256,128]{1,0:T(8,128)(2,1)S(1)} %broadcast_select_fusion.11, bf16[384,128]{1,0:T(8,128)(2,1)S(1)} %broadcast_select_fusion.1, bf16[384,128]{1,0:T(8,128)(2,1)S(1)} %broadcast_select_fusion.6, ...), kind=kOutput, calls=%fused_computation.31 | convolution fusion | flops 269746176 | bytes 2818049 | tf_op jit(solution)/shard_map/dot_general | solution.py:49
  44.8 0.2 collective-permute-start.14
  45.0 1.2 %collective-permute-start.12 = (bf16[384,128]{1,0:T(8,128)(2,1)S(1)}, bf16[384,128]{1,0:T(8,128)(2,1)S(1)}, u32[]{:S(2)}, u32[]{:S(2)}) collective-permute-start(bf16[384,128]{1,0:T(8,128)(2,1)S(1)} %get-tuple-element.17), channel_id=1, source_target_pairs={{0,4},{1,5},{2,6},{3,7},{4,8},{5,9},{6,10},{7,11},{8,12},{9,13},{1... | collective-permute-start | bytes 294920 | tf_op jit(solution)/shard_map/ppermute | solution.py:16
  46.2 1.8 %collective-permute-start.13 = (bf16[384,128]{1,0:T(8,128)(2,1)S(1)}, bf16[384,128]{1,0:T(8,128)(2,1)S(1)}, u32[]{:S(2)}, u32[]{:S(2)}) collective-permute-start(bf16[384,128]{1,0:T(8,128)(2,1)S(1)} %get-tuple-element.18), channel_id=1, source_target_pairs={{0,1},{1,2},{2,3},{3,0},{4,5},{5,6},{6,7},{7,4},{8,9},{9,10},{10,1... | collective-permute-start | bytes 294920 | tf_op jit(solution)/shard_map/ppermute | solution.py:16
  48.0 4.3 %collective-permute-done.14 = bf16[256,128]{1,0:T(8,128)(2,1)S(1)} collective-permute-done((bf16[256,128]{1,0:T(8,128)(2,1)S(1)}, bf16[256,128]{1,0:T(8,128)(2,1)S(1)}, u32[]{:S(2)}, u32[]{:S(2)}) %collective-permute-start.14) | collective-permute-done | bytes 65568 | tf_op jit(solution)/shard_map/ppermute | solution.py:16
  52.3 0.0 collective-permute-done.12
  52.3 0.3 collective-permute-done.13
  52.6 2.1 %fusion.57 = f32[1,1,1024,128]{3,2,1,0:T(8,128)} fusion(bf16[1,1,1024,1024]{3,2,1,0:T(8,128)(2,1)S(1)} %copy-done, bf16[256,128]{1,0:T(8,128)(2,1)S(1)} %broadcast_select_fusion.10, bf16[384,128]{1,0:T(8,128)(2,1)S(1)} %broadcast_select_fusion, bf16[384,128]{1,0:T(8,128)(2,1)S(1)} %broadcast_select_fusion.5, bf16[768,128]{1,0:T(8,128)(2,1)S(1)} %get-tuple-element.11, ...), kind=kOutput, calls=%fused_computation.27 | convolution fusion | flops 269615104 | bytes 3080193 | tf_op jit(solution)/shard_map/dot_general | solution.py:49
  (25 shorter events, 0.3 us)
Async XLA Ops:
  0.0 3.0 %copy-start = (bf16[1,1,1024,1024]{3,2,1,0:T(8,128)(2,1)S(1)}, bf16[1,1,1024,1024]{3,2,1,0:T(8,128)(2,1)}, u32[]{:S(2)}) copy-start(bf16[1,1,1024,1024]{3,2,1,0:T(8,128)(2,1)} %param.4) | copy-start | bytes 6291460
  0.0 2.2 %copy-start.2 = (s32[6]{0:T(128)S(1)}, s32[6]{0:T(128)}, u32[]{:S(2)}) copy-start(s32[6]{0:T(128)} %param.7) | copy-start | bytes 76
  0.0 3.0 %copy-start.1 = (f32[1,1,1024,128]{3,2,1,0:T(8,128)S(1)}, f32[1,1,1024,128]{3,2,1,0:T(8,128)}, u32[]{:S(2)}) copy-start(f32[1,1,1024,128]{3,2,1,0:T(8,128)} %param.6) | copy-start | bytes 1572868
  4.4 8.5 %collective-permute-start.2 = (bf16[256,128]{1,0:T(8,128)(2,1)S(1)}, bf16[256,128]{1,0:T(8,128)(2,1)S(1)}, u32[]{:S(2)}, u32[]{:S(2)}) collective-permute-start(bf16[256,128]{1,0:T(8,128)(2,1)S(1)} %slice.86), channel_id=1, source_target_pairs={{0,5},{1,6},{2,7},{3,4},{4,9},{5,10},{6,11},{7,8},{8,13},{9,14},{1... | collective-permute-start | bytes 196616 | tf_op jit(solution)/shard_map/ppermute | solution.py:16
  6.9 6.5 %collective-permute-start = (bf16[384,128]{1,0:T(8,128)(2,1)S(1)}, bf16[384,128]{1,0:T(8,128)(2,1)S(1)}, u32[]{:S(2)}, u32[]{:S(2)}) collective-permute-start(bf16[384,128]{1,0:T(8,128)(2,1)S(1)} %get-tuple-element.25), channel_id=1, source_target_pairs={{0,4},{1,5},{2,6},{3,7},{4,8},{5,9},{6,10},{7,11},{8,12},{9,13},{1... | collective-permute-start | bytes 294920 | tf_op jit(solution)/shard_map/ppermute | solution.py:16
  8.6 6.3 %collective-permute-start.1 = (bf16[384,128]{1,0:T(8,128)(2,1)S(1)}, bf16[384,128]{1,0:T(8,128)(2,1)S(1)}, u32[]{:S(2)}, u32[]{:S(2)}) collective-permute-start(bf16[384,128]{1,0:T(8,128)(2,1)S(1)} %get-tuple-element.26), channel_id=1, source_target_pairs={{0,1},{1,2},{2,3},{3,0},{4,5},{5,6},{6,7},{7,4},{8,9},{9,10},{10,1... | collective-permute-start | bytes 294920 | tf_op jit(solution)/shard_map/ppermute | solution.py:16
  17.2 7.4 %collective-permute-start.5 = (bf16[256,128]{1,0:T(8,128)(2,1)S(1)}, bf16[256,128]{1,0:T(8,128)(2,1)S(1)}, u32[]{:S(2)}, u32[]{:S(2)}) collective-permute-start(bf16[256,128]{1,0:T(8,128)(2,1)S(1)} %slice.89), channel_id=1, source_target_pairs={{0,5},{1,6},{2,7},{3,4},{4,9},{5,10},{6,11},{7,8},{8,13},{9,14},{1... | collective-permute-start | bytes 196616 | tf_op jit(solution)/shard_map/ppermute | solution.py:16
  17.3 7.4 %collective-permute-start.3 = (bf16[384,128]{1,0:T(8,128)(2,1)S(1)}, bf16[384,128]{1,0:T(8,128)(2,1)S(1)}, u32[]{:S(2)}, u32[]{:S(2)}) collective-permute-start(bf16[384,128]{1,0:T(8,128)(2,1)S(1)} %get-tuple-element.23), channel_id=1, source_target_pairs={{0,4},{1,5},{2,6},{3,7},{4,8},{5,9},{6,10},{7,11},{8,12},{9,13},{1... | collective-permute-start | bytes 294920 | tf_op jit(solution)/shard_map/ppermute | solution.py:16
  18.4 6.4 %collective-permute-start.4 = (bf16[384,128]{1,0:T(8,128)(2,1)S(1)}, bf16[384,128]{1,0:T(8,128)(2,1)S(1)}, u32[]{:S(2)}, u32[]{:S(2)}) collective-permute-start(bf16[384,128]{1,0:T(8,128)(2,1)S(1)} %get-tuple-element.24), channel_id=1, source_target_pairs={{0,1},{1,2},{2,3},{3,0},{4,5},{5,6},{6,7},{7,4},{8,9},{9,10},{10,1... | collective-permute-start | bytes 294920 | tf_op jit(solution)/shard_map/ppermute | solution.py:16
  26.2 7.4 %collective-permute-start.8 = (bf16[256,128]{1,0:T(8,128)(2,1)S(1)}, bf16[256,128]{1,0:T(8,128)(2,1)S(1)}, u32[]{:S(2)}, u32[]{:S(2)}) collective-permute-start(bf16[256,128]{1,0:T(8,128)(2,1)S(1)} %slice.92), channel_id=1, source_target_pairs={{0,5},{1,6},{2,7},{3,4},{4,9},{5,10},{6,11},{7,8},{8,13},{9,14},{1... | collective-permute-start | bytes 196616 | tf_op jit(solution)/shard_map/ppermute | solution.py:16
  27.2 6.5 %collective-permute-start.6 = (bf16[384,128]{1,0:T(8,128)(2,1)S(1)}, bf16[384,128]{1,0:T(8,128)(2,1)S(1)}, u32[]{:S(2)}, u32[]{:S(2)}) collective-permute-start(bf16[384,128]{1,0:T(8,128)(2,1)S(1)} %get-tuple-element.21), channel_id=1, source_target_pairs={{0,4},{1,5},{2,6},{3,7},{4,8},{5,9},{6,10},{7,11},{8,12},{9,13},{1... | collective-permute-start | bytes 294920 | tf_op jit(solution)/shard_map/ppermute | solution.py:16
  28.2 6.4 %collective-permute-start.7 = (bf16[384,128]{1,0:T(8,128)(2,1)S(1)}, bf16[384,128]{1,0:T(8,128)(2,1)S(1)}, u32[]{:S(2)}, u32[]{:S(2)}) collective-permute-start(bf16[384,128]{1,0:T(8,128)(2,1)S(1)} %get-tuple-element.22), channel_id=1, source_target_pairs={{0,1},{1,2},{2,3},{3,0},{4,5},{5,6},{6,7},{7,4},{8,9},{9,10},{10,1... | collective-permute-start | bytes 294920 | tf_op jit(solution)/shard_map/ppermute | solution.py:16
  36.0 7.4 %collective-permute-start.11 = (bf16[256,128]{1,0:T(8,128)(2,1)S(1)}, bf16[256,128]{1,0:T(8,128)(2,1)S(1)}, u32[]{:S(2)}, u32[]{:S(2)}) collective-permute-start(bf16[256,128]{1,0:T(8,128)(2,1)S(1)} %slice.95), channel_id=1, source_target_pairs={{0,5},{1,6},{2,7},{3,4},{4,9},{5,10},{6,11},{7,8},{8,13},{9,14},{1... | collective-permute-start | bytes 196616 | tf_op jit(solution)/shard_map/ppermute | solution.py:16
  36.1 7.3 %collective-permute-start.9 = (bf16[384,128]{1,0:T(8,128)(2,1)S(1)}, bf16[384,128]{1,0:T(8,128)(2,1)S(1)}, u32[]{:S(2)}, u32[]{:S(2)}) collective-permute-start(bf16[384,128]{1,0:T(8,128)(2,1)S(1)} %get-tuple-element.19), channel_id=1, source_target_pairs={{0,4},{1,5},{2,6},{3,7},{4,8},{5,9},{6,10},{7,11},{8,12},{9,13},{1... | collective-permute-start | bytes 294920 | tf_op jit(solution)/shard_map/ppermute | solution.py:16
  37.0 6.4 %collective-permute-start.10 = (bf16[384,128]{1,0:T(8,128)(2,1)S(1)}, bf16[384,128]{1,0:T(8,128)(2,1)S(1)}, u32[]{:S(2)}, u32[]{:S(2)}) collective-permute-start(bf16[384,128]{1,0:T(8,128)(2,1)S(1)} %get-tuple-element.20), channel_id=1, source_target_pairs={{0,1},{1,2},{2,3},{3,0},{4,5},{5,6},{6,7},{7,4},{8,9},{9,10},{10,1... | collective-permute-start | bytes 294920 | tf_op jit(solution)/shard_map/ppermute | solution.py:16
  44.8 7.4 %collective-permute-start.14 = (bf16[256,128]{1,0:T(8,128)(2,1)S(1)}, bf16[256,128]{1,0:T(8,128)(2,1)S(1)}, u32[]{:S(2)}, u32[]{:S(2)}) collective-permute-start(bf16[256,128]{1,0:T(8,128)(2,1)S(1)} %slice.98), channel_id=1, source_target_pairs={{0,5},{1,6},{2,7},{3,4},{4,9},{5,10},{6,11},{7,8},{8,13},{9,14},{1... | collective-permute-start | bytes 196616 | tf_op jit(solution)/shard_map/ppermute | solution.py:16
  45.0 7.3 %collective-permute-start.12 = (bf16[384,128]{1,0:T(8,128)(2,1)S(1)}, bf16[384,128]{1,0:T(8,128)(2,1)S(1)}, u32[]{:S(2)}, u32[]{:S(2)}) collective-permute-start(bf16[384,128]{1,0:T(8,128)(2,1)S(1)} %get-tuple-element.17), channel_id=1, source_target_pairs={{0,4},{1,5},{2,6},{3,7},{4,8},{5,9},{6,10},{7,11},{8,12},{9,13},{1... | collective-permute-start | bytes 294920 | tf_op jit(solution)/shard_map/ppermute | solution.py:16
  46.2 6.4 %collective-permute-start.13 = (bf16[384,128]{1,0:T(8,128)(2,1)S(1)}, bf16[384,128]{1,0:T(8,128)(2,1)S(1)}, u32[]{:S(2)}, u32[]{:S(2)}) collective-permute-start(bf16[384,128]{1,0:T(8,128)(2,1)S(1)} %get-tuple-element.18), channel_id=1, source_target_pairs={{0,1},{1,2},{2,3},{3,0},{4,5},{5,6},{6,7},{7,4},{8,9},{9,10},{10,1... | collective-permute-start | bytes 294920 | tf_op jit(solution)/shard_map/ppermute | solution.py:16

commit v2 on v0

v2 whole, which is shorter than its diff:
```python
import random

import jax
import jax.numpy as jnp
from jax import lax
from jax.sharding import PartitionSpec as P

AXES = ("gx", "gy")


def distance(mesh, a, b):
    devices = mesh.devices.flat
    place = []
    for k in (a, b):
        coords = getattr(devices[k], "coords", None)
        place.append(divmod(k, mesh.shape["gy"]) if coords is None else tuple(coords))
    return sum(abs(p - q) for p, q in zip(*place))


def shift_pairs(mesh, dx, dy):
    nx, ny = mesh.shape["gx"], mesh.shape["gy"]
    return [(i * ny + j, (i + dx) % nx * ny + (j + dy) % ny) for i in range(nx) for j in range(ny)]


def diagonal_pairs(mesh):
    nx, ny = mesh.shape["gx"], mesh.shape["gy"]
    inner = [(i * ny + j, (i + 1) * ny + j + 1) for i in range(nx - 1) for j in range(ny - 1)]
    onward = dict(inner)
    arrived = set(onward.values())
    starts = [k for k in range(nx * ny) if k not in arrived]
    ends = []
    for k in starts:
        while k in onward:
            k = onward[k]
        ends.append(k)
    total = len(starts)
    gap = [[distance(mesh, e, s) for s in starts] for e in ends]

    def cost(order):
        hops = [gap[order[k - 1]][order[k]] for k in range(total)]
        return max(hops), sum(h * h for h in hops)

    draw = random.Random(1)
    best = None
    for _ in range(max(1, 6000 // total**2)):
        order = list(range(total))
        draw.shuffle(order)
        current = cost(order)
        moved = True
        while moved:
            moved = False
            for a in range(total):
                for b in range(a + 1, total):
                    swapped = order[:]
                    swapped[a], swapped[b] = swapped[b], swapped[a]
                    slid = order[:a] + order[a + 1 : b + 1] + [order[a]] + order[b + 1 :]
                    for trial in (swapped, slid):
                        value = cost(trial)
                        if value < current:
                            order, current, moved = trial, value, True
        if best is None or current < best[0]:
            best = current, order
    order = best[1]
    return inner + [(ends[order[k - 1]], starts[order[k]]) for k in range(total)]


def after(value, *others):
    return lax.optimization_barrier((value, *others))[0]


def local(pairs, green, sources, entering, start_front):
    operator = green[0, 0]
    tick_total = sources.shape[0]
    order = operator.shape[0]
    edge_rows = sources.shape[3]
    trace_rows = edge_rows // 2
    width = entering.shape[3]
    column, row = lax.axis_index("gx"), lax.axis_index("gy")
    column_total, row_total = lax.axis_size("gx"), lax.axis_size("gy")
    front_index = column + row
    rows = {"east": slice(0, trace_rows), "north": slice(trace_rows, edge_rows), "corner": slice(edge_rows, order)}
    has_target = {"east": column < column_total - 1, "north": row < row_total - 1}
    has_target["corner"] = has_target["east"] & has_target["north"]
    has_source = {"east": column > 0, "north": row > 0}
    has_source["corner"] = has_source["east"] & has_source["north"]

    def times(matrix, vectors):
        return jnp.dot(matrix, vectors, preferred_element_type=jnp.float32)

    def source_term(step_index):
        edges = sources[step_index, 0, 0].astype(jnp.float32)
        return jnp.concatenate([edges, jnp.zeros((order - edge_rows, width), jnp.float32)], axis=0)

    def kept(condition, value):
        return jnp.where(condition, value, jnp.zeros_like(value))

    first = times(operator, entering[0, 0].astype(jnp.bfloat16)) + source_term(0)
    first = first.astype(jnp.bfloat16)
    outgoing = {name: first[rows[name]] for name in ("corner", "east", "north")}

    span = max(tick_total, 3)
    age = front_index - after(start_front, outgoing["north"])
    live_bits = lax.reduce(
        jnp.where((age >= 0) & (age < span), lax.shift_left(jnp.int32(1), jnp.clip(age, 0, span - 1)), 0),
        jnp.int32(0),
        lax.bitwise_or,
        (0,),
    )
    live_bits = live_bits | (front_index << span)

    def live(step_index):
        return (lax.shift_right_logical(live_bits, jnp.int32(step_index)) & 1) == 1

    for step_index in range(1, tick_total):
        arrived = {name: lax.ppermute(outgoing[name], AXES, pairs[name]) for name in ("corner", "east", "north")}
        if step_index == 1:
            has_source["corner"] = has_source["corner"] & live(2)
            arrived = {name: kept(has_source[name], value) for name, value in arrived.items()}
        partial = source_term(step_index)
        for name in ("east", "corner"):
            partial = partial + times(operator[:, rows[name]], arrived[name])
        if step_index == tick_total - 1:
            total = times(operator[:, rows["north"]], arrived["north"]) + partial
            return kept(live(step_index), total)[None, None]
        outgoing, previous = {}, arrived["north"]
        for name in ("corner", "east", "north"):
            product = times(operator[rows[name], rows["north"]], previous) + partial[rows[name]]
            sent = has_target[name] & live(step_index) if name == "corner" else has_target[name]
            outgoing[name] = kept(sent, product).astype(jnp.bfloat16)
            previous = after(arrived["north"], outgoing[name])


def solution(mesh):
    pairs = {
        "east": shift_pairs(mesh, 1, 0),
        "north": shift_pairs(mesh, 0, 1),
        "corner": diagonal_pairs(mesh),
    }
    in_specs = (
        P("gx", "gy", None, None),
        P(None, "gx", "gy", None, None),
        P("gx", "gy", None, None),
        P(),
    )

    def body(*shards):
        return local(pairs, *shards)

    return jax.shard_map(body, mesh=mesh, in_specs=in_specs, out_specs=P("gx", "gy", None, None), check_vma=False)
```

time: 84 us -> 50.1 us (0.60)
  starting transfers between devices: 62.3 us -> 20.2 us
  waiting for transfers between devices: 9.36 us -> 14.7 us
  local copies, waits for them, and re-layouts: 1.68 us -> 5.09 us
    ppermute x20 -> x15, starting transfers between devices: 62.3 us -> 20.2 us  [local(): lax.ppermute(outgoing[name], AXES, pairs[name])]
    ppermute x20 -> x15, waiting for transfers between devices: 9.36 us -> 14.7 us  [local(): lax.ppermute(outgoing[name], AXES, pairs[name])]
    slice x10 -> x3, local copies, waits for them, and re-layouts: 0.11 us -> 2.87 us  [the longest x1 1.55 us: source_term(): edges = sources[step_index, 0, 0].astype(jnp.float32)]
    convert_element_type x1 -> x0, local copies, waits for them, and re-layouts: 1.56 us -> none  [local(): sources[step_index, 0, 0].astype(jnp.float32)]
    unnamed x6 -> x9, local copies, waits for them, and re-layouts: 0.01 us -> 1.22 us
    broadcast_in_dim x0 -> x1, local copies, waits for them, and re-layouts: none -> 1 us  [local(): return kept(live(step_index), total)[None, None]]
    dot_general x6 -> x24, matrix products: 8.77 us -> 8.4 us  [times(): return jnp.dot(matrix, vectors, preferred_element_type=jnp.float32)]
  transfers between devices with their start and end apart: 20 -> 15, of which waited for: 5 -> 13; matrix products, arithmetic and copies ran while one was open for 0% -> 14% of each run, Pallas kernels for 0% -> 0%
where the time goes in v2:
time: 50.1 us; the launch traced here: 49.9 us
  starting transfers between devices  20.2 us (40%)
  waiting for transfers between devices  14.7 us (29%)
  matrix products  8.4 us (17%)
  local copies, waits for them, and re-layouts  5.09 us (10%)
  between operations  0.87 us (2%)
  other arithmetic  0.65 us (1%)
    ppermute x15, starting transfers between devices, local(): lax.ppermute(outgoing[name], AXES, pairs[name])  20.2 us
    ppermute x15, waiting for transfers between devices, local(): lax.ppermute(outgoing[name], AXES, pairs[name])  14.7 us
    dot_general x24, matrix products, times(): return jnp.dot(matrix, vectors, preferred_element_type=jnp.float32)  8.4 us
    slice x1, local copies, waits for them, and re-layouts, source_term(): edges = sources[step_index, 0, 0].astype(jnp.float32)  1.55 us
    slice x2, local copies, waits for them, and re-layouts, local(): outgoing = {name: first[rows[name]] for name in ('corner', 'east', 'north')}  1.31 us
    unnamed x9, local copies, waits for them, and re-layouts  1.22 us
  transfers between devices with their start and end apart: 15, of which 13 were waited for; matrix products, arithmetic and copies ran while one was open for 14% of the time, Pallas kernels for 0%

profile of v2, /device:TPU:0, one launch (start us, length us, event | category | flops | bytes accessed | tf_op | source)
XLA Modules:
  0.0 49.9 jit_solution(4343532618129875127)
XLA Ops:
  0.0 1.6 %fusion.85 = (bf16[1,1,1,768,128]{4,3,2,1,0:T(8,128)(2,1)S(1)}, bf16[1,1,1,768,128]{4,3,2,1,0:T(8,128)(2,1)S(1)}, bf16[1,1,1,768,128]{4,3,2,1,0:T(8,128)(2,1)S(1...) fusion(bf16[6,1,1,768,128]{4,3,2,1,0:T(8,128)(2,1)} %param.5), kind=kLoop, calls=%fused_computation.112 | loop fusion | bytes 2359296 | tf_op jit(solution)/shard_map/slice | solution.py:91
  1.6 0.5 copy-done
  2.1 1.8 %fusion.13 = bf16[1024,128]{1,0:T(8,128)(2,1)S(1)} fusion(bf16[768,128]{1,0:T(8,128)(2,1)S(1)} %get-tuple-element.28, f32[1,1,1024,128]{3,2,1,0:T(8,128)} %param.6, bf16[1,1,1024,1024]{3,2,1,0:T(8,128)(2,1)S(1)} %copy-done), kind=kOutput, calls=%fused_computation.25 | convolution fusion | flops 268959744 | bytes 3080192 | tf_op jit(solution)/shard_map/dot_general | solution.py:88
  3.8 0.6 %slice.129 = bf16[256,128]{1,0:T(8,128)(2,1)} slice(bf16[1024,128]{1,0:T(8,128)(2,1)S(1)} %fusion.13), slice={[768:1024], [0:128]} | slice | bytes 131072 | tf_op jit(solution)/shard_map/slice | solution.py:99
  4.4 2.4 %collective-permute-start.2 = (bf16[256,128]{1,0:T(8,128)(2,1)}, bf16[256,128]{1,0:T(8,128)(2,1)S(1)}, u32[]{:S(2)}, u32[]{:S(2)}) collective-permute-start(bf16[256,128]{1,0:T(8,128)(2,1)} %slice.129), channel_id=1, source_target_pairs={{0,5},{1,6},{2,7},{4,9},{5,10},{6,11},{8,13},{9,14},{10,15},{12,17... | collective-permute-start | bytes 196616 | tf_op jit(solution)/shard_map/ppermute | solution.py:115
  6.9 0.7 %fusion.86 = (bf16[384,128]{1,0:T(8,128)(2,1)}, bf16[384,128]{1,0:T(8,128)(2,1)}) fusion(bf16[1024,128]{1,0:T(8,128)(2,1)S(1)} %fusion.13), kind=kLoop, calls=%fused_computation.113 | loop fusion | bytes 393216 | tf_op jit(solution)/shard_map/slice | solution.py:99
  7.5 1.7 %collective-permute-start.1 = (bf16[384,128]{1,0:T(8,128)(2,1)}, bf16[384,128]{1,0:T(8,128)(2,1)S(1)}, u32[]{:S(2)}, u32[]{:S(2)}) collective-permute-start(bf16[384,128]{1,0:T(8,128)(2,1)} %get-tuple-element.29), channel_id=1, source_target_pairs={{0,4},{1,5},{2,6},{3,7},{4,8},{5,9},{6,10},{7,11},{8,12},{9,13},{1... | collective-permute-start | bytes 294920 | tf_op jit(solution)/shard_map/ppermute | solution.py:115
  9.2 1.5 %collective-permute-start = (bf16[384,128]{1,0:T(8,128)(2,1)}, bf16[384,128]{1,0:T(8,128)(2,1)S(1)}, u32[]{:S(2)}, u32[]{:S(2)}) collective-permute-start(bf16[384,128]{1,0:T(8,128)(2,1)} %get-tuple-element.30), channel_id=1, source_target_pairs={{0,1},{1,2},{2,3},{3,0},{4,5},{5,6},{6,7},{7,4},{8,9},{9,10},{10,1... | collective-permute-start | bytes 294920 | tf_op jit(solution)/shard_map/ppermute | solution.py:115
  10.7 0.1 copy.15
  10.9 0.1 copy.14
  11.0 0.1 copy.13
  11.2 0.1 copy.12
  11.3 0.1 copy.11
  11.5 0.6 %fusion.81 = s32[]{:T(128)} fusion(s32[6]{0:T(128)S(1)} %copy-done.1, s32[]{:T(128)S(6)} %add.87), kind=kLoop, calls=%fused_computation.108 | loop fusion | flops 47 | bytes 32 | tf_op jit(solution)/shard_map/reduce | solution.py:103
  12.7 0.3 convolution_bitcast_fusion.4
  13.0 2.0 %collective-permute-done = bf16[384,128]{1,0:T(8,128)(2,1)S(1)} collective-permute-done((bf16[384,128]{1,0:T(8,128)(2,1)}, bf16[384,128]{1,0:T(8,128)(2,1)S(1)}, u32[]{:S(2)}, u32[]{:S(2)}) %collective-permute-start) | collective-permute-done | bytes 98336 | tf_op jit(solution)/shard_map/ppermute | solution.py:115
  15.1 0.0 collective-permute-done.1
  15.1 0.4 fusion.12
  15.5 0.2 fusion.49
  15.7 0.1 collective-permute-start.5
  15.8 0.3 fusion.30
  16.1 1.8 %collective-permute-start.4 = (bf16[384,128]{0,1:T(8,128)(2,1)S(1)}, bf16[384,128]{0,1:T(8,128)(2,1)S(1)}, u32[]{:S(2)}, u32[]{:S(2)}) collective-permute-start(bf16[384,128]{0,1:T(8,128)(2,1)S(1)} %fusion.30), channel_id=1, source_target_pairs={{0,4},{1,5},{2,6},{3,7},{4,8},{5,9},{6,10},{7,11},{8,12},{9,13},{1... | collective-permute-start | bytes 294920 | tf_op jit(solution)/shard_map/ppermute | solution.py:115
  17.8 0.3 fusion.31
  18.1 2.4 %collective-permute-start.3 = (bf16[384,128]{0,1:T(8,128)(2,1)S(1)}, bf16[384,128]{0,1:T(8,128)(2,1)S(1)}, u32[]{:S(2)}, u32[]{:S(2)}) collective-permute-start(bf16[384,128]{0,1:T(8,128)(2,1)S(1)} %fusion.31), channel_id=1, source_target_pairs={{0,1},{1,2},{2,3},{3,0},{4,5},{5,6},{6,7},{7,4},{8,9},{9,10},{10,1... | collective-permute-start | bytes 294920 | tf_op jit(solution)/shard_map/ppermute | solution.py:115
  20.5 0.4 collective-permute-done.5
  20.9 0.3 convolution_bitcast_fusion.3
  21.3 0.7 %collective-permute-done.4 = bf16[384,128]{0,1:T(8,128)(2,1)S(1)} collective-permute-done((bf16[384,128]{0,1:T(8,128)(2,1)S(1)}, bf16[384,128]{0,1:T(8,128)(2,1)S(1)}, u32[]{:S(2)}, u32[]{:S(2)}) %collective-permute-start.4) | collective-permute-done | bytes 98336 | tf_op jit(solution)/shard_map/ppermute | solution.py:115
  21.9 0.4 fusion.10
  22.3 1.7 %collective-permute-done.3 = bf16[384,128]{0,1:T(8,128)(2,1)S(1)} collective-permute-done((bf16[384,128]{0,1:T(8,128)(2,1)S(1)}, bf16[384,128]{0,1:T(8,128)(2,1)S(1)}, u32[]{:S(2)}, u32[]{:S(2)}) %collective-permute-start.3) | collective-permute-done | bytes 98336 | tf_op jit(solution)/shard_map/ppermute | solution.py:115
  24.0 0.2 fusion.48
  24.2 0.1 collective-permute-start.8
  24.3 0.2 fusion.32
  24.5 2.4 %collective-permute-start.7 = (bf16[384,128]{0,1:T(8,128)(2,1)S(1)}, bf16[384,128]{0,1:T(8,128)(2,1)S(1)}, u32[]{:S(2)}, u32[]{:S(2)}) collective-permute-start(bf16[384,128]{0,1:T(8,128)(2,1)S(1)} %fusion.32), channel_id=1, source_target_pairs={{0,4},{1,5},{2,6},{3,7},{4,8},{5,9},{6,10},{7,11},{8,12},{9,13},{1... | collective-permute-start | bytes 294920 | tf_op jit(solution)/shard_map/ppermute | solution.py:115
  26.9 0.2 fusion.33
  27.2 1.5 %collective-permute-start.6 = (bf16[384,128]{0,1:T(8,128)(2,1)S(1)}, bf16[384,128]{0,1:T(8,128)(2,1)S(1)}, u32[]{:S(2)}, u32[]{:S(2)}) collective-permute-start(bf16[384,128]{0,1:T(8,128)(2,1)S(1)} %fusion.33), channel_id=1, source_target_pairs={{0,1},{1,2},{2,3},{3,0},{4,5},{5,6},{6,7},{7,4},{8,9},{9,10},{10,1... | collective-permute-start | bytes 294920 | tf_op jit(solution)/shard_map/ppermute | solution.py:115
  28.7 0.7 %collective-permute-done.8 = bf16[256,128]{0,1:T(8,128)(2,1)S(1)} collective-permute-done((bf16[256,128]{0,1:T(8,128)(2,1)S(1)}, bf16[256,128]{0,1:T(8,128)(2,1)S(1)}, u32[]{:S(2)}, u32[]{:S(2)}) %collective-permute-start.8) | collective-permute-done | bytes 65568 | tf_op jit(solution)/shard_map/ppermute | solution.py:115
  29.4 0.3 convolution_bitcast_fusion.2
  29.7 0.7 %collective-permute-done.7 = bf16[384,128]{0,1:T(8,128)(2,1)S(1)} collective-permute-done((bf16[384,128]{0,1:T(8,128)(2,1)S(1)}, bf16[384,128]{0,1:T(8,128)(2,1)S(1)}, u32[]{:S(2)}, u32[]{:S(2)}) %collective-permute-start.7) | collective-permute-done | bytes 98336 | tf_op jit(solution)/shard_map/ppermute | solution.py:115
  30.4 0.4 fusion.8
  30.8 2.0 %collective-permute-done.6 = bf16[384,128]{0,1:T(8,128)(2,1)S(1)} collective-permute-done((bf16[384,128]{0,1:T(8,128)(2,1)S(1)}, bf16[384,128]{0,1:T(8,128)(2,1)S(1)}, u32[]{:S(2)}, u32[]{:S(2)}) %collective-permute-start.6) | collective-permute-done | bytes 98336 | tf_op jit(solution)/shard_map/ppermute | solution.py:115
  32.8 0.2 fusion.47
  33.1 0.1 collective-permute-start.11
  33.1 0.2 fusion.34
  33.4 1.1 %collective-permute-start.10 = (bf16[384,128]{0,1:T(8,128)(2,1)S(1)}, bf16[384,128]{0,1:T(8,128)(2,1)S(1)}, u32[]{:S(2)}, u32[]{:S(2)}) collective-permute-start(bf16[384,128]{0,1:T(8,128)(2,1)S(1)} %fusion.34), channel_id=1, source_target_pairs={{0,4},{1,5},{2,6},{3,7},{4,8},{5,9},{6,10},{7,11},{8,12},{9,13},{1... | collective-permute-start | bytes 294920 | tf_op jit(solution)/shard_map/ppermute | solution.py:115
  34.5 0.2 fusion.35
  34.7 1.8 %collective-permute-start.9 = (bf16[384,128]{0,1:T(8,128)(2,1)S(1)}, bf16[384,128]{0,1:T(8,128)(2,1)S(1)}, u32[]{:S(2)}, u32[]{:S(2)}) collective-permute-start(bf16[384,128]{0,1:T(8,128)(2,1)S(1)} %fusion.35), channel_id=1, source_target_pairs={{0,1},{1,2},{2,3},{3,0},{4,5},{5,6},{6,7},{7,4},{8,9},{9,10},{10,1... | collective-permute-start | bytes 294920 | tf_op jit(solution)/shard_map/ppermute | solution.py:115
  36.6 1.7 %collective-permute-done.11 = bf16[256,128]{0,1:T(8,128)(2,1)S(1)} collective-permute-done((bf16[256,128]{0,1:T(8,128)(2,1)S(1)}, bf16[256,128]{0,1:T(8,128)(2,1)S(1)}, u32[]{:S(2)}, u32[]{:S(2)}) %collective-permute-start.11) | collective-permute-done | bytes 65568 | tf_op jit(solution)/shard_map/ppermute | solution.py:115
  38.3 0.3 convolution_bitcast_fusion.1
  38.6 0.7 %collective-permute-done.10 = bf16[384,128]{0,1:T(8,128)(2,1)S(1)} collective-permute-done((bf16[384,128]{0,1:T(8,128)(2,1)S(1)}, bf16[384,128]{0,1:T(8,128)(2,1)S(1)}, u32[]{:S(2)}, u32[]{:S(2)}) %collective-permute-start.10) | collective-permute-done | bytes 98336 | tf_op jit(solution)/shard_map/ppermute | solution.py:115
  39.3 0.4 fusion.6
  39.7 0.7 %collective-permute-done.9 = bf16[384,128]{0,1:T(8,128)(2,1)S(1)} collective-permute-done((bf16[384,128]{0,1:T(8,128)(2,1)S(1)}, bf16[384,128]{0,1:T(8,128)(2,1)S(1)}, u32[]{:S(2)}, u32[]{:S(2)}) %collective-permute-start.9) | collective-permute-done | bytes 98336 | tf_op jit(solution)/shard_map/ppermute | solution.py:115
  40.4 0.2 fusion.46
  40.6 0.1 collective-permute-start.14
  40.7 0.2 fusion.36
  40.9 1.7 %collective-permute-start.13 = (bf16[384,128]{0,1:T(8,128)(2,1)S(1)}, bf16[384,128]{0,1:T(8,128)(2,1)S(1)}, u32[]{:S(2)}, u32[]{:S(2)}) collective-permute-start(bf16[384,128]{0,1:T(8,128)(2,1)S(1)} %fusion.36), channel_id=1, source_target_pairs={{0,4},{1,5},{2,6},{3,7},{4,8},{5,9},{6,10},{7,11},{8,12},{9,13},{1... | collective-permute-start | bytes 294920 | tf_op jit(solution)/shard_map/ppermute | solution.py:115
  42.6 0.2 fusion.37
  42.8 1.6 %collective-permute-start.12 = (bf16[384,128]{0,1:T(8,128)(2,1)S(1)}, bf16[384,128]{0,1:T(8,128)(2,1)S(1)}, u32[]{:S(2)}, u32[]{:S(2)}) collective-permute-start(bf16[384,128]{0,1:T(8,128)(2,1)S(1)} %fusion.37), channel_id=1, source_target_pairs={{0,1},{1,2},{2,3},{3,0},{4,5},{5,6},{6,7},{7,4},{8,9},{9,10},{10,1... | collective-permute-start | bytes 294920 | tf_op jit(solution)/shard_map/ppermute | solution.py:115
  44.4 1.4 %collective-permute-done.14 = bf16[256,128]{0,1:T(8,128)(2,1)S(1)} collective-permute-done((bf16[256,128]{0,1:T(8,128)(2,1)S(1)}, bf16[256,128]{0,1:T(8,128)(2,1)S(1)}, u32[]{:S(2)}, u32[]{:S(2)}) %collective-permute-start.14) | collective-permute-done | bytes 65568 | tf_op jit(solution)/shard_map/ppermute | solution.py:115
  45.9 0.3 convolution_bitcast_fusion
  46.2 0.7 %collective-permute-done.13 = bf16[384,128]{0,1:T(8,128)(2,1)S(1)} collective-permute-done((bf16[384,128]{0,1:T(8,128)(2,1)S(1)}, bf16[384,128]{0,1:T(8,128)(2,1)S(1)}, u32[]{:S(2)}, u32[]{:S(2)}) %collective-permute-start.13) | collective-permute-done | bytes 98336 | tf_op jit(solution)/shard_map/ppermute | solution.py:115
  46.8 0.4 fusion.1
  47.2 1.3 %collective-permute-done.12 = bf16[384,128]{0,1:T(8,128)(2,1)S(1)} collective-permute-done((bf16[384,128]{0,1:T(8,128)(2,1)S(1)}, bf16[384,128]{0,1:T(8,128)(2,1)S(1)}, u32[]{:S(2)}, u32[]{:S(2)}) %collective-permute-start.12) | collective-permute-done | bytes 98336 | tf_op jit(solution)/shard_map/ppermute | solution.py:115
  48.5 0.4 fusion.4
  48.9 1.0 %copy.10 = f32[1,1,1024,128]{3,2,1,0:T(8,128)} copy(f32[1,1,1024,128]{2,3,1,0:T(8,128)S(1)} %fusion.4) | data formatting | bytes 1048576 | tf_op jit(solution)/shard_map/broadcast_in_dim | solution.py:124
  (5 shorter events, 0.0 us)
Async XLA Ops:
  0.0 2.0 %copy-start = (bf16[1,1,1024,1024]{3,2,1,0:T(8,128)(2,1)S(1)}, bf16[1,1,1024,1024]{3,2,1,0:T(8,128)(2,1)}, u32[]{:S(2)}) copy-start(bf16[1,1,1024,1024]{3,2,1,0:T(8,128)(2,1)} %param.4) | copy-start | bytes 6291460
  2.0 9.4 %copy-start.1 = (s32[6]{0:T(128)S(1)}, s32[6]{0:T(128)}, u32[]{:S(2)}) copy-start(s32[6]{0:T(128)} %param.7) | copy-start | bytes 76
  4.4 8.3 %collective-permute-start.2 = (bf16[256,128]{1,0:T(8,128)(2,1)}, bf16[256,128]{1,0:T(8,128)(2,1)S(1)}, u32[]{:S(2)}, u32[]{:S(2)}) collective-permute-start(bf16[256,128]{1,0:T(8,128)(2,1)} %slice.129), channel_id=1, source_target_pairs={{0,5},{1,6},{2,7},{4,9},{5,10},{6,11},{8,13},{9,14},{10,15},{12,17... | collective-permute-start | bytes 196616 | tf_op jit(solution)/shard_map/ppermute | solution.py:115
  7.5 7.5 %collective-permute-start.1 = (bf16[384,128]{1,0:T(8,128)(2,1)}, bf16[384,128]{1,0:T(8,128)(2,1)S(1)}, u32[]{:S(2)}, u32[]{:S(2)}) collective-permute-start(bf16[384,128]{1,0:T(8,128)(2,1)} %get-tuple-element.29), channel_id=1, source_target_pairs={{0,4},{1,5},{2,6},{3,7},{4,8},{5,9},{6,10},{7,11},{8,12},{9,13},{1... | collective-permute-start | bytes 294920 | tf_op jit(solution)/shard_map/ppermute | solution.py:115
  9.2 5.8 %collective-permute-start = (bf16[384,128]{1,0:T(8,128)(2,1)}, bf16[384,128]{1,0:T(8,128)(2,1)S(1)}, u32[]{:S(2)}, u32[]{:S(2)}) collective-permute-start(bf16[384,128]{1,0:T(8,128)(2,1)} %get-tuple-element.30), channel_id=1, source_target_pairs={{0,1},{1,2},{2,3},{3,0},{4,5},{5,6},{6,7},{7,4},{8,9},{9,10},{10,1... | collective-permute-start | bytes 294920 | tf_op jit(solution)/shard_map/ppermute | solution.py:115
  15.7 5.2 %collective-permute-start.5 = (bf16[256,128]{0,1:T(8,128)(2,1)S(1)}, bf16[256,128]{0,1:T(8,128)(2,1)S(1)}, u32[]{:S(2)}, u32[]{:S(2)}) collective-permute-start(bf16[256,128]{0,1:T(8,128)(2,1)S(1)} %fusion.49), channel_id=1, source_target_pairs={{0,5},{1,6},{2,7},{4,9},{5,10},{6,11},{8,13},{9,14},{10,15},{12,17... | collective-permute-start | bytes 196616 | tf_op jit(solution)/shard_map/ppermute | solution.py:115
  16.1 5.9 %collective-permute-start.4 = (bf16[384,128]{0,1:T(8,128)(2,1)S(1)}, bf16[384,128]{0,1:T(8,128)(2,1)S(1)}, u32[]{:S(2)}, u32[]{:S(2)}) collective-permute-start(bf16[384,128]{0,1:T(8,128)(2,1)S(1)} %fusion.30), channel_id=1, source_target_pairs={{0,4},{1,5},{2,6},{3,7},{4,8},{5,9},{6,10},{7,11},{8,12},{9,13},{1... | collective-permute-start | bytes 294920 | tf_op jit(solution)/shard_map/ppermute | solution.py:115
  18.1 5.9 %collective-permute-start.3 = (bf16[384,128]{0,1:T(8,128)(2,1)S(1)}, bf16[384,128]{0,1:T(8,128)(2,1)S(1)}, u32[]{:S(2)}, u32[]{:S(2)}) collective-permute-start(bf16[384,128]{0,1:T(8,128)(2,1)S(1)} %fusion.31), channel_id=1, source_target_pairs={{0,1},{1,2},{2,3},{3,0},{4,5},{5,6},{6,7},{7,4},{8,9},{9,10},{10,1... | collective-permute-start | bytes 294920 | tf_op jit(solution)/shard_map/ppermute | solution.py:115
  24.2 5.2 %collective-permute-start.8 = (bf16[256,128]{0,1:T(8,128)(2,1)S(1)}, bf16[256,128]{0,1:T(8,128)(2,1)S(1)}, u32[]{:S(2)}, u32[]{:S(2)}) collective-permute-start(bf16[256,128]{0,1:T(8,128)(2,1)S(1)} %fusion.48), channel_id=1, source_target_pairs={{0,5},{1,6},{2,7},{4,9},{5,10},{6,11},{8,13},{9,14},{10,15},{12,17... | collective-permute-start | bytes 196616 | tf_op jit(solution)/shard_map/ppermute | solution.py:115
  24.5 5.9 %collective-permute-start.7 = (bf16[384,128]{0,1:T(8,128)(2,1)S(1)}, bf16[384,128]{0,1:T(8,128)(2,1)S(1)}, u32[]{:S(2)}, u32[]{:S(2)}) collective-permute-start(bf16[384,128]{0,1:T(8,128)(2,1)S(1)} %fusion.32), channel_id=1, source_target_pairs={{0,4},{1,5},{2,6},{3,7},{4,8},{5,9},{6,10},{7,11},{8,12},{9,13},{1... | collective-permute-start | bytes 294920 | tf_op jit(solution)/shard_map/ppermute | solution.py:115
  27.2 5.7 %collective-permute-start.6 = (bf16[384,128]{0,1:T(8,128)(2,1)S(1)}, bf16[384,128]{0,1:T(8,128)(2,1)S(1)}, u32[]{:S(2)}, u32[]{:S(2)}) collective-permute-start(bf16[384,128]{0,1:T(8,128)(2,1)S(1)} %fusion.33), channel_id=1, source_target_pairs={{0,1},{1,2},{2,3},{3,0},{4,5},{5,6},{6,7},{7,4},{8,9},{9,10},{10,1... | collective-permute-start | bytes 294920 | tf_op jit(solution)/shard_map/ppermute | solution.py:115
  33.1 5.2 %collective-permute-start.11 = (bf16[256,128]{0,1:T(8,128)(2,1)S(1)}, bf16[256,128]{0,1:T(8,128)(2,1)S(1)}, u32[]{:S(2)}, u32[]{:S(2)}) collective-permute-start(bf16[256,128]{0,1:T(8,128)(2,1)S(1)} %fusion.47), channel_id=1, source_target_pairs={{0,5},{1,6},{2,7},{4,9},{5,10},{6,11},{8,13},{9,14},{10,15},{12,17... | collective-permute-start | bytes 196616 | tf_op jit(solution)/shard_map/ppermute | solution.py:115
  33.4 5.9 %collective-permute-start.10 = (bf16[384,128]{0,1:T(8,128)(2,1)S(1)}, bf16[384,128]{0,1:T(8,128)(2,1)S(1)}, u32[]{:S(2)}, u32[]{:S(2)}) collective-permute-start(bf16[384,128]{0,1:T(8,128)(2,1)S(1)} %fusion.34), channel_id=1, source_target_pairs={{0,4},{1,5},{2,6},{3,7},{4,8},{5,9},{6,10},{7,11},{8,12},{9,13},{1... | collective-permute-start | bytes 294920 | tf_op jit(solution)/shard_map/ppermute | solution.py:115
  34.7 5.7 %collective-permute-start.9 = (bf16[384,128]{0,1:T(8,128)(2,1)S(1)}, bf16[384,128]{0,1:T(8,128)(2,1)S(1)}, u32[]{:S(2)}, u32[]{:S(2)}) collective-permute-start(bf16[384,128]{0,1:T(8,128)(2,1)S(1)} %fusion.35), channel_id=1, source_target_pairs={{0,1},{1,2},{2,3},{3,0},{4,5},{5,6},{6,7},{7,4},{8,9},{9,10},{10,1... | collective-permute-start | bytes 294920 | tf_op jit(solution)/shard_map/ppermute | solution.py:115
  40.6 5.2 %collective-permute-start.14 = (bf16[256,128]{0,1:T(8,128)(2,1)S(1)}, bf16[256,128]{0,1:T(8,128)(2,1)S(1)}, u32[]{:S(2)}, u32[]{:S(2)}) collective-permute-start(bf16[256,128]{0,1:T(8,128)(2,1)S(1)} %fusion.46), channel_id=1, source_target_pairs={{0,5},{1,6},{2,7},{4,9},{5,10},{6,11},{8,13},{9,14},{10,15},{12,17... | collective-permute-start | bytes 196616 | tf_op jit(solution)/shard_map/ppermute | solution.py:115
  40.9 5.9 %collective-permute-start.13 = (bf16[384,128]{0,1:T(8,128)(2,1)S(1)}, bf16[384,128]{0,1:T(8,128)(2,1)S(1)}, u32[]{:S(2)}, u32[]{:S(2)}) collective-permute-start(bf16[384,128]{0,1:T(8,128)(2,1)S(1)} %fusion.36), channel_id=1, source_target_pairs={{0,4},{1,5},{2,6},{3,7},{4,8},{5,9},{6,10},{7,11},{8,12},{9,13},{1... | collective-permute-start | bytes 294920 | tf_op jit(solution)/shard_map/ppermute | solution.py:115
  42.8 5.7 %collective-permute-start.12 = (bf16[384,128]{0,1:T(8,128)(2,1)S(1)}, bf16[384,128]{0,1:T(8,128)(2,1)S(1)}, u32[]{:S(2)}, u32[]{:S(2)}) collective-permute-start(bf16[384,128]{0,1:T(8,128)(2,1)S(1)} %fusion.37), channel_id=1, source_target_pairs={{0,1},{1,2},{2,3},{3,0},{4,5},{5,6},{6,7},{7,4},{8,9},{9,10},{10,1... | collective-permute-start | bytes 294920 | tf_op jit(solution)/shard_map/ppermute | solution.py:115

commit v3 on v2

--- a/solution.py
+++ b/solution.py
@@ -3,9 +3,12 @@
 import jax
 import jax.numpy as jnp
 from jax import lax
+from jax.experimental import pallas as pl
+from jax.experimental.pallas import tpu as pltpu
 from jax.sharding import PartitionSpec as P
 
 AXES = ("gx", "gy")
+SENT = ("corner", "east", "north")
 
 
 def distance(mesh, a, b):
@@ -68,35 +71,102 @@
     return lax.optimization_barrier((value, *others))[0]
 
 
+def trace_slices(order, edge_rows):
+    trace_rows = edge_rows // 2
+    return {
+        "east": slice(0, trace_rows),
+        "north": slice(trace_rows, edge_rows),
+        "corner": slice(edge_rows, order),
+    }
+
+
+def targets():
+    east = lax.axis_index("gx") < lax.axis_size("gx") - 1
+    north = lax.axis_index("gy") < lax.axis_size("gy") - 1
+    return {"east": east, "north": north, "corner": east & north}
+
+
+def first_tick(green, sources, entering):
+    order, width = entering.shape[2:]
+    edge_rows = sources.shape[3]
+    rows = trace_slices(order, edge_rows)
+
+    def kernel(green_hbm, sources_hbm, entering_hbm, corner, east, north, operator, later, edges, wide, narrow, sems):
+        outgoing = {"corner": corner, "east": east, "north": north}
+        has_target = targets()
+
+        def fetch(source, target, k):
+            copy = pltpu.make_async_copy(source, target, sems.at[k])
+            copy.start()
+            return copy
+
+        entering_copy = fetch(entering_hbm.at[0, 0], wide, 0)
+        operator_copies = {}
+        for k, name in enumerate(SENT):
+            part = pl.ds(rows[name].start, rows[name].stop - rows[name].start)
+            operator_copies[name] = fetch(green_hbm.at[0, 0, part], operator.at[part], 1 + k)
+            if k == 0:
+                edges_copy = fetch(sources_hbm.at[0, 0, 0], edges, 1 + len(SENT))
+        later_copy = fetch(sources_hbm.at[1, 0, 0], later, 2 + len(SENT))
+        entering_copy.wait()
+        narrow[...] = wide[...].astype(jnp.bfloat16)
+        for name in SENT:
+            operator_copies[name].wait()
+            product = jnp.dot(operator[rows[name]], narrow[...], preferred_element_type=jnp.float32)
+            if name == SENT[1]:
+                edges_copy.wait()
+            if name != "corner":
+                product = product + edges[rows[name]].astype(jnp.float32)
+            outgoing[name][...] = jnp.where(has_target[name], product, 0.0).astype(jnp.bfloat16)
+        later_copy.wait()
+
+    count = {name: rows[name].stop - rows[name].start for name in SENT}
+    results = [jax.ShapeDtypeStruct((count[name], width), jnp.bfloat16) for name in SENT]
+    results += [jax.ShapeDtypeStruct((order, order), jnp.bfloat16), jax.ShapeDtypeStruct((edge_rows, width), jnp.bfloat16)]
+    call = pl.pallas_call(
+        kernel,
+        out_shape=results,
+        in_specs=[pl.BlockSpec(memory_space=pltpu.HBM)] * 3,
+        out_specs=[pl.BlockSpec(memory_space=pltpu.VMEM)] * len(results),
+        scratch_shapes=[
+            pltpu.VMEM((edge_rows, width), jnp.bfloat16),
+            pltpu.VMEM((order, width), jnp.float32),
+            pltpu.VMEM((order, width), jnp.bfloat16),
+            pltpu.SemaphoreType.DMA((3 + len(SENT),)),
+        ],
+        compiler_params=pltpu.CompilerParams(vmem_limit_bytes=46_000_000),
+        cost_estimate=pl.CostEstimate(
+            flops=2 * order * order * width,
+            bytes_accessed=2 * order * order + 4 * order * width + 4 * edge_rows * width,
+            transcendentals=0,
+        ),
+        name="first_tick",
+    )
+    in_hbm = [pltpu.with_memory_space_constraint(value, pltpu.HBM) for value in (green, sources, entering)]
+    *outgoing, operator, later = call(*in_hbm)
+    return dict(zip(SENT, outgoing)), operator, later
+
+
 def local(pairs, green, sources, entering, start_front):
-    operator = green[0, 0]
     tick_total = sources.shape[0]
-    order = operator.shape[0]
+    order, width = entering.shape[2:]
     edge_rows = sources.shape[3]
-    trace_rows = edge_rows // 2
-    width = entering.shape[3]
-    column, row = lax.axis_index("gx"), lax.axis_index("gy")
-    column_total, row_total = lax.axis_size("gx"), lax.axis_size("gy")
-    front_index = column + row
-    rows = {"east": slice(0, trace_rows), "north": slice(trace_rows, edge_rows), "corner": slice(edge_rows, order)}
-    has_target = {"east": column < column_total - 1, "north": row < row_total - 1}
-    has_target["corner"] = has_target["east"] & has_target["north"]
-    has_source = {"east": column > 0, "north": row > 0}
-    has_source["corner"] = has_source["east"] & has_source["north"]
+    rows = trace_slices(order, edge_rows)
+    front_index = lax.axis_index("gx") + lax.axis_index("gy")
+    has_target = targets()
 
     def times(matrix, vectors):
         return jnp.dot(matrix, vectors, preferred_element_type=jnp.float32)
 
-    def source_term(step_index):
-        edges = sources[step_index, 0, 0].astype(jnp.float32)
-        return jnp.concatenate([edges, jnp.zeros((order - edge_rows, width), jnp.float32)], axis=0)
+    def source_term(edges):
+        return jnp.concatenate(
+            [edges.astype(jnp.float32), jnp.zeros((order - edge_rows, width), jnp.float32)], axis=0
+        )
 
     def kept(condition, value):
         return jnp.where(condition, value, jnp.zeros_like(value))
 
-    first = times(operator, entering[0, 0].astype(jnp.bfloat16)) + source_term(0)
-    first = first.astype(jnp.bfloat16)
-    outgoing = {name: first[rows[name]] for name in ("corner", "east", "north")}
+    outgoing, operator, second_edges = first_tick(green, sources, entering)
 
     span = max(tick_total, 3)
     age = front_index - after(start_front, outgoing["north"])
@@ -107,23 +177,23 @@
         (0,),
     )
     live_bits = live_bits | (front_index << span)
+    later_sources = after(sources, outgoing["north"])
 
     def live(step_index):
         return (lax.shift_right_logical(live_bits, jnp.int32(step_index)) & 1) == 1
 
     for step_index in range(1, tick_total):
-        arrived = {name: lax.ppermute(outgoing[name], AXES, pairs[name]) for name in ("corner", "east", "north")}
+        arrived = {name: lax.ppermute(outgoing[name], AXES, pairs[name]) for name in SENT}
         if step_index == 1:
-            has_source["corner"] = has_source["corner"] & live(2)
-            arrived = {name: kept(has_source[name], value) for name, value in arrived.items()}
-        partial = source_term(step_index)
+            arrived["corner"] = kept(live(2), arrived["corner"])
+        partial = source_term(second_edges if step_index == 1 else later_sources[step_index, 0, 0])
         for name in ("east", "corner"):
             partial = partial + times(operator[:, rows[name]], arrived[name])
         if step_index == tick_total - 1:
             total = times(operator[:, rows["north"]], arrived["north"]) + partial
             return kept(live(step_index), total)[None, None]
         outgoing, previous = {}, arrived["north"]
-        for name in ("corner", "east", "north"):
+        for name in SENT:
             product = times(operator[rows[name], rows["north"]], previous) + partial[rows[name]]
             sent = has_target[name] & live(step_index) if name == "corner" else has_target[name]
             outgoing[name] = kept(sent, product).astype(jnp.bfloat16)

time: 50.1 us -> 47.2 us (0.942)
  local copies, waits for them, and re-layouts: 5.09 us -> 1.28 us
  Pallas kernels: 0 us -> 2.77 us
  starting transfers between devices: 20.2 us -> 19 us
    slice x3 -> x0, local copies, waits for them, and re-layouts: 2.87 us -> none  [the longest x1 1.55 us: source_term(): edges = sources[step_index, 0, 0].astype(jnp.float32)]
    pallas_call x0 -> x1, Pallas kernels: none -> 2.77 us  [first_tick(): *outgoing, operator, later = call(*in_hbm)]
    convert_element_type x0 -> x1, local copies, waits for them, and re-layouts: none -> 1.27 us  [source_term(): edges.astype(jnp.float32)]
    unnamed x9 -> x2, local copies, waits for them, and re-layouts: 1.22 us -> 0.01 us
    ppermute x15, starting transfers between devices: 20.2 us -> 19 us  [local(): lax.ppermute(outgoing[name], AXES, pairs[name])]
    broadcast_in_dim x1 -> x0, local copies, waits for them, and re-layouts: 1 us -> none  [local(): return kept(live(step_index), total)[None, None]]
    dot_general x24 -> x23, matrix products: 8.4 us -> 8.1 us  [times(): return jnp.dot(matrix, vectors, preferred_element_type=jnp.float32)]
  transfers between devices with their start and end apart: 15 -> 15, of which waited for: 13 -> 12; matrix products, arithmetic and copies ran while one was open for 14% -> 17% of each run, Pallas kernels for 0% -> 0%
where the time goes in v3:
time: 47.2 us; the launch traced here: 46.9 us
  starting transfers between devices  19 us (40%)
  waiting for transfers between devices  14.2 us (30%)
  matrix products  8.1 us (17%)
  Pallas kernels  2.77 us (6%)
  local copies, waits for them, and re-layouts  1.28 us (3%)
  between operations  0.93 us (2%)
  other arithmetic  0.64 us (1%)
    ppermute x15, starting transfers between devices, local(): lax.ppermute(outgoing[name], AXES, pairs[name])  19 us
    ppermute x15, waiting for transfers between devices, local(): lax.ppermute(outgoing[name], AXES, pairs[name])  14.2 us
    dot_general x23, matrix products, times(): return jnp.dot(matrix, vectors, preferred_element_type=jnp.float32)  8.1 us
    pallas_call x1, Pallas kernels, first_tick(): *outgoing, operator, later = call(*in_hbm)  2.77 us
    convert_element_type x1, local copies, waits for them, and re-layouts, source_term(): edges.astype(jnp.float32)  1.27 us
  transfers between devices with their start and end apart: 15, of which 12 were waited for; matrix products, arithmetic and copies ran while one was open for 17% of the time, Pallas kernels for 0%

profile of v3, /device:TPU:0, one launch (start us, length us, event | category | flops | bytes accessed | tf_op | source)
XLA Modules:
  0.0 46.9 jit_solution(17902898242244890670)
XLA Ops:
  0.0 0.0 copy-start
  0.0 2.8 %first_tick.1 = (bf16[256,128]{1,0:T(8,128)(2,1)S(1)}, bf16[384,128]{1,0:T(8,128)(2,1)S(1)}, bf16[384,128]{1,0:T(8,128)(2,1)S(1)}, bf16[1024,1024]{1,0:T(8,128)(2,1)S(1)}, bf16[768,128]{1,0:T(8,128)(2,1)S(1)}) custom-call(bf16[1,1,1024,1024]{3,2,1,0:T(8,128)(2,1)} %green_hbm.1, bf16[6,1,1,768,128]{4,3,2,1,0:T(8,128)(2,1)} %sources_hbm.1, ...), custom_call_target="tpu_custom_call" | custom-call | flops 268435456 | bytes 3014656 | tf_op jit(solution)/shard_map/first_tick/pallas_call | solution.py:146
  2.8 2.5 %collective-permute-start.2 = (bf16[256,128]{1,0:T(8,128)(2,1)S(1)}, bf16[256,128]{1,0:T(8,128)(2,1)}, u32[]{:S(2)}, u32[]{:S(2)}) collective-permute-start(bf16[256,128]{1,0:T(8,128)(2,1)S(1)} %get-tuple-element.25), channel_id=1, source_target_pairs={{0,5},{1,6},{2,7},{4,9},{5,10},{6,11},{8,13},{9,14},{10,15},{12,17... | collective-permute-start | bytes 196616 | tf_op jit(solution)/shard_map/ppermute | solution.py:186
  5.2 1.7 %collective-permute-start.1 = (bf16[384,128]{1,0:T(8,128)(2,1)S(1)}, bf16[384,128]{1,0:T(8,128)(2,1)S(1)}, u32[]{:S(2)}, u32[]{:S(2)}) collective-permute-start(bf16[384,128]{1,0:T(8,128)(2,1)S(1)} %get-tuple-element.24), channel_id=1, source_target_pairs={{0,4},{1,5},{2,6},{3,7},{4,8},{5,9},{6,10},{7,11},{8,12},{9,13},{1... | collective-permute-start | bytes 294920 | tf_op jit(solution)/shard_map/ppermute | solution.py:186
  6.9 1.5 %collective-permute-start = (bf16[384,128]{1,0:T(8,128)(2,1)S(1)}, bf16[384,128]{1,0:T(8,128)(2,1)S(1)}, u32[]{:S(2)}, u32[]{:S(2)}) collective-permute-start(bf16[384,128]{1,0:T(8,128)(2,1)S(1)} %get-tuple-element.20), channel_id=1, source_target_pairs={{0,1},{1,2},{2,3},{3,0},{4,5},{5,6},{6,7},{7,4},{8,9},{9,10},{10,1... | collective-permute-start | bytes 294920 | tf_op jit(solution)/shard_map/ppermute | solution.py:186
  8.4 1.3 %slice_bitcast_fusion = (bf16[768,128]{1,0:T(8,128)(2,1)S(1)}, bf16[768,128]{1,0:T(8,128)(2,1)S(1)}, bf16[768,128]{1,0:T(8,128)(2,1)S(1)}, bf16[768,128]{1,0:T(8,128)(2,1)S(1)}) fusion(bf16[6,1,1,768,128]{4,3,2,1,0:T(8,128)(2,1)} %sources_hbm.1), kind=kLoop, calls=%fused_computation.65 | loop fusion | bytes 1572864 | tf_op jit(solution)/shard_map/convert_element_type | solution.py:163
  9.7 0.0 copy-done
  9.7 0.6 %fusion.62 = s32[]{:T(128)} fusion(s32[6]{0:T(128)S(1)} %copy-done, s32[]{:T(128)S(6)} %add.82), kind=kLoop, calls=%fused_computation.85 | loop fusion | flops 47 | bytes 32 | tf_op jit(solution)/shard_map/reduce | solution.py:173
  11.0 0.0 collective-permute-done.2
  11.0 1.1 %fusion.45 = f32[1024,128]{1,0:T(8,128)S(1)} fusion(bf16[1024,1024]{1,0:T(8,128)(2,1)S(1)} %get-tuple-element.22, bf16[256,128]{1,0:T(8,128)(2,1)} %collective-permute-done.2, pred[]{:T(512)S(6)} %eq.18), kind=kOutput, calls=%fused_computation.63 | convolution fusion | flops 67141632 | bytes 1114113 | tf_op jit(solution)/shard_map/dot_general | solution.py:159
  12.2 0.0 collective-permute-done.1
  12.2 0.4 fusion.6
  12.6 0.0 collective-permute-done
  12.6 0.2 fusion.27
  12.8 0.1 collective-permute-start.5
  12.9 0.2 fusion.15
  13.1 1.8 %collective-permute-start.4 = (bf16[384,128]{1,0:T(8,128)(2,1)S(1)}, bf16[384,128]{1,0:T(8,128)(2,1)S(1)}, u32[]{:S(2)}, u32[]{:S(2)}) collective-permute-start(bf16[384,128]{1,0:T(8,128)(2,1)S(1)} %fusion.15), channel_id=1, source_target_pairs={{0,4},{1,5},{2,6},{3,7},{4,8},{5,9},{6,10},{7,11},{8,12},{9,13},{1... | collective-permute-start | bytes 294920 | tf_op jit(solution)/shard_map/ppermute | solution.py:186
  14.9 0.2 fusion.16
  15.2 2.3 %collective-permute-start.3 = (bf16[384,128]{1,0:T(8,128)(2,1)S(1)}, bf16[384,128]{1,0:T(8,128)(2,1)S(1)}, u32[]{:S(2)}, u32[]{:S(2)}) collective-permute-start(bf16[384,128]{1,0:T(8,128)(2,1)S(1)} %fusion.16), channel_id=1, source_target_pairs={{0,1},{1,2},{2,3},{3,0},{4,5},{5,6},{6,7},{7,4},{8,9},{9,10},{10,1... | collective-permute-start | bytes 294920 | tf_op jit(solution)/shard_map/ppermute | solution.py:186
  17.5 0.5 %collective-permute-done.5 = bf16[256,128]{1,0:T(8,128)(2,1)S(1)} collective-permute-done((bf16[256,128]{1,0:T(8,128)(2,1)S(1)}, bf16[256,128]{1,0:T(8,128)(2,1)S(1)}, u32[]{:S(2)}, u32[]{:S(2)}) %collective-permute-start.5) | collective-permute-done | bytes 65568 | tf_op jit(solution)/shard_map/ppermute | solution.py:186
  18.0 0.3 fusion.43
  18.3 0.7 %collective-permute-done.4 = bf16[384,128]{1,0:T(8,128)(2,1)S(1)} collective-permute-done((bf16[384,128]{1,0:T(8,128)(2,1)S(1)}, bf16[384,128]{1,0:T(8,128)(2,1)S(1)}, u32[]{:S(2)}, u32[]{:S(2)}) %collective-permute-start.4) | collective-permute-done | bytes 98336 | tf_op jit(solution)/shard_map/ppermute | solution.py:186
  19.0 0.4 fusion.5
  19.4 2.2 %collective-permute-done.3 = bf16[384,128]{1,0:T(8,128)(2,1)S(1)} collective-permute-done((bf16[384,128]{1,0:T(8,128)(2,1)S(1)}, bf16[384,128]{1,0:T(8,128)(2,1)S(1)}, u32[]{:S(2)}, u32[]{:S(2)}) %collective-permute-start.3) | collective-permute-done | bytes 98336 | tf_op jit(solution)/shard_map/ppermute | solution.py:186
  21.6 0.2 fusion.28
  21.8 0.1 collective-permute-start.8
  21.8 0.2 fusion.17
  22.1 1.8 %collective-permute-start.7 = (bf16[384,128]{1,0:T(8,128)(2,1)S(1)}, bf16[384,128]{1,0:T(8,128)(2,1)S(1)}, u32[]{:S(2)}, u32[]{:S(2)}) collective-permute-start(bf16[384,128]{1,0:T(8,128)(2,1)S(1)} %fusion.17), channel_id=1, source_target_pairs={{0,4},{1,5},{2,6},{3,7},{4,8},{5,9},{6,10},{7,11},{8,12},{9,13},{1... | collective-permute-start | bytes 294920 | tf_op jit(solution)/shard_map/ppermute | solution.py:186
  23.9 0.2 fusion.18
  24.2 1.5 %collective-permute-start.6 = (bf16[384,128]{1,0:T(8,128)(2,1)S(1)}, bf16[384,128]{1,0:T(8,128)(2,1)S(1)}, u32[]{:S(2)}, u32[]{:S(2)}) collective-permute-start(bf16[384,128]{1,0:T(8,128)(2,1)S(1)} %fusion.18), channel_id=1, source_target_pairs={{0,1},{1,2},{2,3},{3,0},{4,5},{5,6},{6,7},{7,4},{8,9},{9,10},{10,1... | collective-permute-start | bytes 294920 | tf_op jit(solution)/shard_map/ppermute | solution.py:186
  25.7 1.3 %collective-permute-done.8 = bf16[256,128]{1,0:T(8,128)(2,1)S(1)} collective-permute-done((bf16[256,128]{1,0:T(8,128)(2,1)S(1)}, bf16[256,128]{1,0:T(8,128)(2,1)S(1)}, u32[]{:S(2)}, u32[]{:S(2)}) %collective-permute-start.8) | collective-permute-done | bytes 65568 | tf_op jit(solution)/shard_map/ppermute | solution.py:186
  27.0 0.3 fusion.41
  27.3 0.7 %collective-permute-done.7 = bf16[384,128]{1,0:T(8,128)(2,1)S(1)} collective-permute-done((bf16[384,128]{1,0:T(8,128)(2,1)S(1)}, bf16[384,128]{1,0:T(8,128)(2,1)S(1)}, u32[]{:S(2)}, u32[]{:S(2)}) %collective-permute-start.7) | collective-permute-done | bytes 98336 | tf_op jit(solution)/shard_map/ppermute | solution.py:186
  28.0 0.4 fusion.4
  28.4 1.6 %collective-permute-done.6 = bf16[384,128]{1,0:T(8,128)(2,1)S(1)} collective-permute-done((bf16[384,128]{1,0:T(8,128)(2,1)S(1)}, bf16[384,128]{1,0:T(8,128)(2,1)S(1)}, u32[]{:S(2)}, u32[]{:S(2)}) %collective-permute-start.6) | collective-permute-done | bytes 98336 | tf_op jit(solution)/shard_map/ppermute | solution.py:186
  30.0 0.2 fusion.29
  30.2 0.1 collective-permute-start.11
  30.3 0.2 fusion.19
  30.5 1.3 %collective-permute-start.10 = (bf16[384,128]{1,0:T(8,128)(2,1)S(1)}, bf16[384,128]{1,0:T(8,128)(2,1)S(1)}, u32[]{:S(2)}, u32[]{:S(2)}) collective-permute-start(bf16[384,128]{1,0:T(8,128)(2,1)S(1)} %fusion.19), channel_id=1, source_target_pairs={{0,4},{1,5},{2,6},{3,7},{4,8},{5,9},{6,10},{7,11},{8,12},{9,13},{1... | collective-permute-start | bytes 294920 | tf_op jit(solution)/shard_map/ppermute | solution.py:186
  31.8 0.2 fusion.20
  32.0 1.5 %collective-permute-start.9 = (bf16[384,128]{1,0:T(8,128)(2,1)S(1)}, bf16[384,128]{1,0:T(8,128)(2,1)S(1)}, u32[]{:S(2)}, u32[]{:S(2)}) collective-permute-start(bf16[384,128]{1,0:T(8,128)(2,1)S(1)} %fusion.20), channel_id=1, source_target_pairs={{0,1},{1,2},{2,3},{3,0},{4,5},{5,6},{6,7},{7,4},{8,9},{9,10},{10,1... | collective-permute-start | bytes 294920 | tf_op jit(solution)/shard_map/ppermute | solution.py:186
  33.5 1.9 %collective-permute-done.11 = bf16[256,128]{1,0:T(8,128)(2,1)S(1)} collective-permute-done((bf16[256,128]{1,0:T(8,128)(2,1)S(1)}, bf16[256,128]{1,0:T(8,128)(2,1)S(1)}, u32[]{:S(2)}, u32[]{:S(2)}) %collective-permute-start.11) | collective-permute-done | bytes 65568 | tf_op jit(solution)/shard_map/ppermute | solution.py:186
  35.4 0.3 fusion.39
  35.7 0.7 %collective-permute-done.10 = bf16[384,128]{1,0:T(8,128)(2,1)S(1)} collective-permute-done((bf16[384,128]{1,0:T(8,128)(2,1)S(1)}, bf16[384,128]{1,0:T(8,128)(2,1)S(1)}, u32[]{:S(2)}, u32[]{:S(2)}) %collective-permute-start.10) | collective-permute-done | bytes 98336 | tf_op jit(solution)/shard_map/ppermute | solution.py:186
  36.4 0.4 fusion.3
  36.8 1.0 %collective-permute-done.9 = bf16[384,128]{1,0:T(8,128)(2,1)S(1)} collective-permute-done((bf16[384,128]{1,0:T(8,128)(2,1)S(1)}, bf16[384,128]{1,0:T(8,128)(2,1)S(1)}, u32[]{:S(2)}, u32[]{:S(2)}) %collective-permute-start.9) | collective-permute-done | bytes 98336 | tf_op jit(solution)/shard_map/ppermute | solution.py:186
  37.8 0.2 fusion.30
  38.0 0.1 collective-permute-start.14
  38.0 0.2 fusion.21
  38.3 1.6 %collective-permute-start.13 = (bf16[384,128]{1,0:T(8,128)(2,1)S(1)}, bf16[384,128]{1,0:T(8,128)(2,1)S(1)}, u32[]{:S(2)}, u32[]{:S(2)}) collective-permute-start(bf16[384,128]{1,0:T(8,128)(2,1)S(1)} %fusion.21), channel_id=1, source_target_pairs={{0,4},{1,5},{2,6},{3,7},{4,8},{5,9},{6,10},{7,11},{8,12},{9,13},{1... | collective-permute-start | bytes 294920 | tf_op jit(solution)/shard_map/ppermute | solution.py:186
  39.8 0.2 fusion.22
  40.1 1.3 %collective-permute-start.12 = (bf16[384,128]{1,0:T(8,128)(2,1)S(1)}, bf16[384,128]{1,0:T(8,128)(2,1)S(1)}, u32[]{:S(2)}, u32[]{:S(2)}) collective-permute-start(bf16[384,128]{1,0:T(8,128)(2,1)S(1)} %fusion.22), channel_id=1, source_target_pairs={{0,1},{1,2},{2,3},{3,0},{4,5},{5,6},{6,7},{7,4},{8,9},{9,10},{10,1... | collective-permute-start | bytes 294920 | tf_op jit(solution)/shard_map/ppermute | solution.py:186
  41.4 1.8 %collective-permute-done.14 = bf16[256,128]{1,0:T(8,128)(2,1)S(1)} collective-permute-done((bf16[256,128]{1,0:T(8,128)(2,1)S(1)}, bf16[256,128]{1,0:T(8,128)(2,1)S(1)}, u32[]{:S(2)}, u32[]{:S(2)}) %collective-permute-start.14) | collective-permute-done | bytes 65568 | tf_op jit(solution)/shard_map/ppermute | solution.py:186
  43.2 0.3 fusion.37
  43.5 0.7 %collective-permute-done.13 = bf16[384,128]{1,0:T(8,128)(2,1)S(1)} collective-permute-done((bf16[384,128]{1,0:T(8,128)(2,1)S(1)}, bf16[384,128]{1,0:T(8,128)(2,1)S(1)}, u32[]{:S(2)}, u32[]{:S(2)}) %collective-permute-start.13) | collective-permute-done | bytes 98336 | tf_op jit(solution)/shard_map/ppermute | solution.py:186
  44.2 0.4 fusion
  44.6 1.2 %collective-permute-done.12 = bf16[384,128]{1,0:T(8,128)(2,1)S(1)} collective-permute-done((bf16[384,128]{1,0:T(8,128)(2,1)S(1)}, bf16[384,128]{1,0:T(8,128)(2,1)S(1)}, u32[]{:S(2)}, u32[]{:S(2)}) %collective-permute-start.12) | collective-permute-done | bytes 98336 | tf_op jit(solution)/shard_map/ppermute | solution.py:186
  45.8 1.2 %fusion.2 = f32[1,1,1024,128]{3,2,1,0:T(8,128)} fusion(f32[1024,128]{1,0:T(8,128)S(1)} %fusion, bf16[384,128]{1,0:T(8,128)(2,1)S(1)} %collective-permute-done.12, bf16[1024,1024]{1,0:T(8,128)(2,1)S(1)} %get-tuple-element.22, pred[]{:T(512)S(6)} %eq.16), kind=kOutput, calls=%fused_computation.4 | convolution fusion | flops 100925440 | bytes 1933313 | tf_op jit(solution)/shard_map/dot_general | solution.py:159
Async XLA Ops:
  0.0 9.7 %copy-start = (s32[6]{0:T(128)S(1)}, s32[6]{0:T(128)}, u32[]{:S(2)}) copy-start(s32[6]{0:T(128)} %param.7) | copy-start | bytes 76
  2.8 8.2 %collective-permute-start.2 = (bf16[256,128]{1,0:T(8,128)(2,1)S(1)}, bf16[256,128]{1,0:T(8,128)(2,1)}, u32[]{:S(2)}, u32[]{:S(2)}) collective-permute-start(bf16[256,128]{1,0:T(8,128)(2,1)S(1)} %get-tuple-element.25), channel_id=1, source_target_pairs={{0,5},{1,6},{2,7},{4,9},{5,10},{6,11},{8,13},{9,14},{10,15},{12,17... | collective-permute-start | bytes 196616 | tf_op jit(solution)/shard_map/ppermute | solution.py:186
  5.2 6.9 %collective-permute-start.1 = (bf16[384,128]{1,0:T(8,128)(2,1)S(1)}, bf16[384,128]{1,0:T(8,128)(2,1)S(1)}, u32[]{:S(2)}, u32[]{:S(2)}) collective-permute-start(bf16[384,128]{1,0:T(8,128)(2,1)S(1)} %get-tuple-element.24), channel_id=1, source_target_pairs={{0,4},{1,5},{2,6},{3,7},{4,8},{5,9},{6,10},{7,11},{8,12},{9,13},{1... | collective-permute-start | bytes 294920 | tf_op jit(solution)/shard_map/ppermute | solution.py:186
  6.9 5.7 %collective-permute-start = (bf16[384,128]{1,0:T(8,128)(2,1)S(1)}, bf16[384,128]{1,0:T(8,128)(2,1)S(1)}, u32[]{:S(2)}, u32[]{:S(2)}) collective-permute-start(bf16[384,128]{1,0:T(8,128)(2,1)S(1)} %get-tuple-element.20), channel_id=1, source_target_pairs={{0,1},{1,2},{2,3},{3,0},{4,5},{5,6},{6,7},{7,4},{8,9},{9,10},{10,1... | collective-permute-start | bytes 294920 | tf_op jit(solution)/shard_map/ppermute | solution.py:186
  12.8 5.2 %collective-permute-start.5 = (bf16[256,128]{1,0:T(8,128)(2,1)S(1)}, bf16[256,128]{1,0:T(8,128)(2,1)S(1)}, u32[]{:S(2)}, u32[]{:S(2)}) collective-permute-start(bf16[256,128]{1,0:T(8,128)(2,1)S(1)} %fusion.27), channel_id=1, source_target_pairs={{0,5},{1,6},{2,7},{4,9},{5,10},{6,11},{8,13},{9,14},{10,15},{12,17... | collective-permute-start | bytes 196616 | tf_op jit(solution)/shard_map/ppermute | solution.py:186
  13.1 5.9 %collective-permute-start.4 = (bf16[384,128]{1,0:T(8,128)(2,1)S(1)}, bf16[384,128]{1,0:T(8,128)(2,1)S(1)}, u32[]{:S(2)}, u32[]{:S(2)}) collective-permute-start(bf16[384,128]{1,0:T(8,128)(2,1)S(1)} %fusion.15), channel_id=1, source_target_pairs={{0,4},{1,5},{2,6},{3,7},{4,8},{5,9},{6,10},{7,11},{8,12},{9,13},{1... | collective-permute-start | bytes 294920 | tf_op jit(solution)/shard_map/ppermute | solution.py:186
  15.2 6.4 %collective-permute-start.3 = (bf16[384,128]{1,0:T(8,128)(2,1)S(1)}, bf16[384,128]{1,0:T(8,128)(2,1)S(1)}, u32[]{:S(2)}, u32[]{:S(2)}) collective-permute-start(bf16[384,128]{1,0:T(8,128)(2,1)S(1)} %fusion.16), channel_id=1, source_target_pairs={{0,1},{1,2},{2,3},{3,0},{4,5},{5,6},{6,7},{7,4},{8,9},{9,10},{10,1... | collective-permute-start | bytes 294920 | tf_op jit(solution)/shard_map/ppermute | solution.py:186
  21.8 5.2 %collective-permute-start.8 = (bf16[256,128]{1,0:T(8,128)(2,1)S(1)}, bf16[256,128]{1,0:T(8,128)(2,1)S(1)}, u32[]{:S(2)}, u32[]{:S(2)}) collective-permute-start(bf16[256,128]{1,0:T(8,128)(2,1)S(1)} %fusion.28), channel_id=1, source_target_pairs={{0,5},{1,6},{2,7},{4,9},{5,10},{6,11},{8,13},{9,14},{10,15},{12,17... | collective-permute-start | bytes 196616 | tf_op jit(solution)/shard_map/ppermute | solution.py:186
  22.1 5.9 %collective-permute-start.7 = (bf16[384,128]{1,0:T(8,128)(2,1)S(1)}, bf16[384,128]{1,0:T(8,128)(2,1)S(1)}, u32[]{:S(2)}, u32[]{:S(2)}) collective-permute-start(bf16[384,128]{1,0:T(8,128)(2,1)S(1)} %fusion.17), channel_id=1, source_target_pairs={{0,4},{1,5},{2,6},{3,7},{4,8},{5,9},{6,10},{7,11},{8,12},{9,13},{1... | collective-permute-start | bytes 294920 | tf_op jit(solution)/shard_map/ppermute | solution.py:186
  24.2 5.9 %collective-permute-start.6 = (bf16[384,128]{1,0:T(8,128)(2,1)S(1)}, bf16[384,128]{1,0:T(8,128)(2,1)S(1)}, u32[]{:S(2)}, u32[]{:S(2)}) collective-permute-start(bf16[384,128]{1,0:T(8,128)(2,1)S(1)} %fusion.18), channel_id=1, source_target_pairs={{0,1},{1,2},{2,3},{3,0},{4,5},{5,6},{6,7},{7,4},{8,9},{9,10},{10,1... | collective-permute-start | bytes 294920 | tf_op jit(solution)/shard_map/ppermute | solution.py:186
  30.2 5.2 %collective-permute-start.11 = (bf16[256,128]{1,0:T(8,128)(2,1)S(1)}, bf16[256,128]{1,0:T(8,128)(2,1)S(1)}, u32[]{:S(2)}, u32[]{:S(2)}) collective-permute-start(bf16[256,128]{1,0:T(8,128)(2,1)S(1)} %fusion.29), channel_id=1, source_target_pairs={{0,5},{1,6},{2,7},{4,9},{5,10},{6,11},{8,13},{9,14},{10,15},{12,17... | collective-permute-start | bytes 196616 | tf_op jit(solution)/shard_map/ppermute | solution.py:186
  30.5 5.9 %collective-permute-start.10 = (bf16[384,128]{1,0:T(8,128)(2,1)S(1)}, bf16[384,128]{1,0:T(8,128)(2,1)S(1)}, u32[]{:S(2)}, u32[]{:S(2)}) collective-permute-start(bf16[384,128]{1,0:T(8,128)(2,1)S(1)} %fusion.19), channel_id=1, source_target_pairs={{0,4},{1,5},{2,6},{3,7},{4,8},{5,9},{6,10},{7,11},{8,12},{9,13},{1... | collective-permute-start | bytes 294920 | tf_op jit(solution)/shard_map/ppermute | solution.py:186
  32.0 5.7 %collective-permute-start.9 = (bf16[384,128]{1,0:T(8,128)(2,1)S(1)}, bf16[384,128]{1,0:T(8,128)(2,1)S(1)}, u32[]{:S(2)}, u32[]{:S(2)}) collective-permute-start(bf16[384,128]{1,0:T(8,128)(2,1)S(1)} %fusion.20), channel_id=1, source_target_pairs={{0,1},{1,2},{2,3},{3,0},{4,5},{5,6},{6,7},{7,4},{8,9},{9,10},{10,1... | collective-permute-start | bytes 294920 | tf_op jit(solution)/shard_map/ppermute | solution.py:186
  38.0 5.2 %collective-permute-start.14 = (bf16[256,128]{1,0:T(8,128)(2,1)S(1)}, bf16[256,128]{1,0:T(8,128)(2,1)S(1)}, u32[]{:S(2)}, u32[]{:S(2)}) collective-permute-start(bf16[256,128]{1,0:T(8,128)(2,1)S(1)} %fusion.30), channel_id=1, source_target_pairs={{0,5},{1,6},{2,7},{4,9},{5,10},{6,11},{8,13},{9,14},{10,15},{12,17... | collective-permute-start | bytes 196616 | tf_op jit(solution)/shard_map/ppermute | solution.py:186
  38.3 5.9 %collective-permute-start.13 = (bf16[384,128]{1,0:T(8,128)(2,1)S(1)}, bf16[384,128]{1,0:T(8,128)(2,1)S(1)}, u32[]{:S(2)}, u32[]{:S(2)}) collective-permute-start(bf16[384,128]{1,0:T(8,128)(2,1)S(1)} %fusion.21), channel_id=1, source_target_pairs={{0,4},{1,5},{2,6},{3,7},{4,8},{5,9},{6,10},{7,11},{8,12},{9,13},{1... | collective-permute-start | bytes 294920 | tf_op jit(solution)/shard_map/ppermute | solution.py:186
  40.1 5.7 %collective-permute-start.12 = (bf16[384,128]{1,0:T(8,128)(2,1)S(1)}, bf16[384,128]{1,0:T(8,128)(2,1)S(1)}, u32[]{:S(2)}, u32[]{:S(2)}) collective-permute-start(bf16[384,128]{1,0:T(8,128)(2,1)S(1)} %fusion.22), channel_id=1, source_target_pairs={{0,1},{1,2},{2,3},{3,0},{4,5},{5,6},{6,7},{7,4},{8,9},{9,10},{10,1... | collective-permute-start | bytes 294920 | tf_op jit(solution)/shard_map/ppermute | solution.py:186
